TPU v7x, 256 devices: a whole 4x4x8 slice. The times are simulated.
256 devices in a mesh: job: 4 (over y), zero: 16 (over z, core), cols: 4 (over x).
Axes of the slice: x: 4, y: 4, z: 8, core: 2. Of those that a mesh axis runs over, the one named last changes fastest.
Arguments:
- weight_query: bfloat16 [12288, 3072], P(('job', 'zero'), 'cols'), parts along dimension 0, may hold values from -0.109375 to 0.109375
- low_query: bfloat16 [12288, 32], P(('job', 'zero')), parts along dimension 0, may hold values from -0.109375 to 0.109375
- high_query: bfloat16 [128, 3072], P('job', 'cols'), parts along dimension 0, may hold values from -1 to 1
- weight_key: bfloat16 [12288, 1024], P(('job', 'zero'), 'cols'), parts along dimension 0, may hold values from -0.109375 to 0.109375
- low_key: bfloat16 [12288, 32], P(('job', 'zero')), parts along dimension 0, may hold values from -0.109375 to 0.109375
- high_key: bfloat16 [128, 1024], P('job', 'cols'), parts along dimension 0, may hold values from -1 to 1
- weight_value: bfloat16 [12288, 1024], P(('job', 'zero'), 'cols'), parts along dimension 0, may hold values from -0.109375 to 0.109375
- low_value: bfloat16 [12288, 32], P(('job', 'zero')), parts along dimension 0, may hold values from -0.109375 to 0.109375
- high_value: bfloat16 [128, 1024], P('job', 'cols'), parts along dimension 0, may hold values from -1 to 1
- weight_mixed: bfloat16 [12288, 3072], P(('job', 'cols'), 'zero'), parts along dimension 0, may hold values from -0.109375 to 0.109375
- low_mixed: bfloat16 [12288, 32], P(('job', 'cols')), parts along dimension 0, may hold values from -0.109375 to 0.109375
- high_mixed: bfloat16 [128, 3072], P('job', 'zero'), parts along dimension 0, may hold values from -1 to 1
- norm_train: float32 [12288], P(('job', 'zero', 'cols')), parts along dimension 0, may hold values from 0.25 to 1.75
- norm_step: float32 [12288], P(('job', 'zero', 'cols')), parts along dimension 0, may hold values from -0.3 to 0.3
Outputs:
- serving_query: bfloat16 [12288, 3072], P('job', 'cols'), parts along dimension 0
- serving_key: bfloat16 [12288, 1024], P('job', 'cols'), parts along dimension 0
- serving_value: bfloat16 [12288, 1024], P('job', 'cols'), parts along dimension 0
- serving_mixed: bfloat16 [12288, 3072], P(('job', 'cols')), parts along dimension 0
- serve_norm: bfloat16 [12288], P('job'), parts along dimension 0
There are 4 independent parts, one for each index of `job`. A program takes and returns all parts, laid end to end along the dimension named above; each array names one. Nothing has to cross between parts.
All inputs are finite; a program needn't handle non-finite values.
Results may differ from a plain program's by a relative error of at most 0.001.
Values may be sent and summed in bfloat16 or wider, within the bound.
A program may use at most 128 MiB of HBM per device.

v0:
```python
import jax
import jax.numpy as jnp
from jax import lax
from jax.sharding import PartitionSpec as P

mix_rate = 2.0


def gather_turned(arrays, axis, dims):
    turned = [jnp.moveaxis(a, dim, 0) for a, dim in zip(arrays, dims)]
    widths = [t[0].size for t in turned]
    both = jnp.concatenate([t.reshape(-1, w) for t, w in zip(turned, widths)], axis=1)
    whole = lax.all_gather(both, axis, axis=0, tiled=True)
    tiles = jnp.split(whole, [sum(widths[:k]) for k in range(1, len(widths))], axis=1)
    return tuple(
        (
            jnp.moveaxis(b.reshape(-1, *t.shape[1:]), 0, dim)
            for b, t, dim in zip(tiles, turned, dims)
        )
    )


def sent_to_all(array, axis):
    copies = jnp.broadcast_to(array, (lax.axis_size(axis), *array.shape))
    return lax.all_to_all(copies, axis, split_axis=0, concat_axis=0, tiled=True)


def joined_along(tiles, dim):
    tiles = jnp.moveaxis(tiles, 0, dim)
    dims = tiles.shape
    return tiles.reshape(*dims[:dim], dims[dim] * dims[dim + 1], *dims[dim + 2 :])


def collect(array, axis, dim):
    tiles = sent_to_all(array, axis)
    return joined_along(tiles, dim)


def on_device(
    weight_query,
    low_query,
    high_query,
    weight_key,
    low_key,
    high_key,
    weight_value,
    low_value,
    high_value,
    weight_mixed,
    low_mixed,
    high_mixed,
    norm_train,
    norm_step,
):
    whole_query = weight_query.astype(jnp.float32) + mix_rate * jnp.dot(
        low_query, high_query, preferred_element_type=jnp.float32
    )
    whole_key = weight_key.astype(jnp.float32) + mix_rate * jnp.dot(
        low_key, high_key, preferred_element_type=jnp.float32
    )
    whole_value = weight_value.astype(jnp.float32) + mix_rate * jnp.dot(
        low_value, high_value, preferred_element_type=jnp.float32
    )
    whole_mixed = weight_mixed.astype(jnp.float32) + mix_rate * jnp.dot(
        low_mixed, high_mixed, preferred_element_type=jnp.float32
    )
    narrow_query, narrow_key, narrow_value, narrow_mixed = (
        whole_query.astype(jnp.bfloat16),
        whole_key.astype(jnp.bfloat16),
        whole_value.astype(jnp.bfloat16),
        whole_mixed.astype(jnp.bfloat16),
    )
    serving_query, serving_key, serving_value, serving_mixed = gather_turned(
        (narrow_query, narrow_key, narrow_value, narrow_mixed), "zero", (0, 0, 0, 1)
    )
    serve_norm = collect((norm_train + norm_step).astype(jnp.bfloat16), ("zero", "cols"), 0)
    return (serving_query, serving_key, serving_value, serving_mixed, serve_norm)


def solution(mesh):
    placed = (
        P(("job", "zero"), "cols"),
        P(("job", "zero"), None),
        P("job", "cols"),
        P(("job", "zero"), "cols"),
        P(("job", "zero"), None),
        P("job", "cols"),
        P(("job", "zero"), "cols"),
        P(("job", "zero"), None),
        P("job", "cols"),
        P(("job", "cols"), "zero"),
        P(("job", "cols"), None),
        P("job", "zero"),
        P(("job", "zero", "cols")),
        P(("job", "zero", "cols")),
    )
    return jax.shard_map(
        on_device,
        mesh=mesh,
        in_specs=placed,
        out_specs=(
            P("job", "cols"),
            P("job", "cols"),
            P("job", "cols"),
            P(("job", "cols"), None),
            P("job"),
        ),
        check_vma=False,
    )
```

profile of v0, /device:TPU:1, one launch (start us, length us, event | category | flops | bytes accessed | tf_op | source)
XLA Modules:
  0.0 119.2 jit_solution(13461833786214713967)
XLA Ops:
  7.2 0.0 copy-start
  7.2 0.0 all-gather.2.cloned.1.call-start
  7.2 0.7 copy-done
  8.0 1.3 %fusion.4 = bf16[192,768]{1,0:T(8,128)(2,1)S(1)} fusion(bf16[768,32]{0,1:T(8,128)(2,1)S(1)} %copy-done, bf16[32,192]{1,0:T(8,128)(2,1)} %param.25, bf16[768,192]{0,1:T(8,128)(2,1)} %param.23), kind=kOutput, calls=%fused_computation.7 | convolution fusion | flops 10027008 | bytes 651264 | tf_op jit(solution)/shard_map/dot_general | solution.py:64
  9.2 1.1 fusion.8
  10.4 0.0 copy-start.1
  10.4 0.0 copy-start.2
  10.4 1.1 fusion.7
  11.6 1.3 %fusion.2 = bf16[192,768]{1,0:T(8,128)(2,1)S(1)} fusion(bf16[192,32]{0,1:T(8,128)(2,1)} %param.15, bf16[32,768]{1,0:T(8,128)(2,1)} %param.16, bf16[192,768]{1,0:T(8,128)(2,1)} %param.14), kind=kOutput, calls=%fused_computation.5 | convolution fusion | flops 10027008 | bytes 651264 | tf_op jit(solution)/shard_map/dot_general | solution.py:55
  12.8 1.0 pad_maximum_fusion
  13.8 0.0 all-gather.2.cloned.1.call-update
  13.8 0.0 copy-done.1
  13.8 0.0 copy-done.2
  13.9 22.0 %all_to_all.6 = bf16[64,1,48]{2,1,0:T(2,128)(2,1)S(1)} all-to-all(bf16[64,1,48]{2,1,0:T(2,128)(2,1)S(1)} %broadcast_in_dim.3), channel_id=1, replica_groups=mesh['job'=4,'zero'=16,'cols'=4] {'zero','cols'}, dimensions={0} | all-to-all | bytes 12288 | tf_op jit(solution)/shard_map/all_to_all | solution.py:25
  35.8 0.1 reduce
  35.9 0.7 reshape.18
  36.6 57.3 %all-gather.2.cloned.1.call-done = bf16[3072,2048]{1,0:T(8,128)(2,1)} async-done(((bf16[192,2048]{1,0:T(8,128)(2,1)}), bf16[3072,2048]{1,0:T(8,128)(2,1)}) %all-gather.2.cloned.1.call-update) | async-done | bytes 12582928 | tf_op jit(solution)/shard_map/all_gather | solution.py:13
  93.9 8.1 %slice_bitcast_fusion = (bf16[768,3072]{0,1:T(8,128)(2,1)}, bf16[3072,768]{1,0:T(8,128)(2,1)}) fusion(bf16[3072,2048]{1,0:T(8,128)(2,1)} %all-gather.2.cloned.1.call-done), kind=kLoop, calls=%fused_computation | loop fusion | bytes 18874368 | tf_op jit(solution)/shard_map/transpose | solution.py:17
  102.0 6.6 %copy.21 = bf16[768,3072]{1,0:T(8,128)(2,1)} copy(bf16[768,3072]{0,1:T(8,128)(2,1)} %get-tuple-element.20) | data formatting | bytes 9437184
  108.6 3.8 %fusion.9 = (bf16[3072,256]{1,0:T(8,128)(2,1)}, bf16[3072,256]{1,0:T(8,128)(2,1)}) fusion(bf16[3072,2048]{1,0:T(8,128)(2,1)} %all-gather.2.cloned.1.call-done), kind=kLoop, calls=%fused_computation.16 | loop fusion | bytes 6291456 | tf_op jit(solution)/shard_map/split | solution.py:14
  (2 shorter events, 0.0 us)
Async XLA Ops:
  7.2 0.8 copy-start
  7.2 86.7 %all-gather.2.cloned.1.call-start = ((), (), s32[]{:S(2)}) async-start(), calls=%async_computation.1 | async-start | bytes 13369344 | tf_op jit(solution)/shard_map/all_gather | solution.py:13
  10.4 3.4 %copy-start.1 = (f32[48]{0:T(128)S(1)}, f32[48]{0:T(128)}, u32[]{:S(2)}) copy-start(f32[48]{0:T(128)} %param.26) | copy-start | bytes 580
  10.4 3.4 %copy-start.2 = (f32[48]{0:T(128)S(1)}, f32[48]{0:T(128)}, u32[]{:S(2)}) copy-start(f32[48]{0:T(128)} %param.27) | copy-start | bytes 580
Sparse Core Ops, SparseCore 0:
  13.9 79.9 all-gather.1
where the time goes:
time: 120 us; the launch traced here: 119 us
  waiting for transfers between devices  57.3 us (48%)
  blocking collectives  22 us (18%)
  local copies, waits for them, and re-layouts  20 us (17%)
  between operations  14.1 us (12%)
  matrix products  4.81 us (4%)
    all_gather x1, waiting for transfers between devices, gather_turned(): whole = lax.all_gather(both, axis, axis=0, tiled=True)  57.3 us
    all_to_all x1, blocking collectives, sent_to_all(): return lax.all_to_all(copies, axis, split_axis=0, concat_axis=0, tiled=True)  22 us
    transpose x1, local copies, waits for them, and re-layouts, gather_turned(): jnp.moveaxis(b.reshape(-1, *t.shape[1:]), 0, dim)  8.13 us
    unnamed x7, local copies, waits for them, and re-layouts  7.37 us
    split x1, local copies, waits for them, and re-layouts, gather_turned(): jnp.split(whole, [sum(widths[:k]) for k in range(1, len(widths))], axis=1)  3.76 us
  transfers between devices with their start and end apart: 1, of which 1 were waited for; matrix products, arithmetic and copies ran while one was open for 1% of the time, Pallas kernels for 0%

commit v1 on v0

v1 whole, which is shorter than its diff:
```python
import functools

import jax
import jax.numpy as jnp
from jax import lax
from jax.experimental import pallas as pl
from jax.experimental.pallas import tpu as pltpu
from jax.sharding import PartitionSpec as P

mix_rate = 2.0
MESH = pl.DeviceIdType.MESH
BF16 = jnp.bfloat16
F32 = jnp.float32

PIECES = ("q0", "q1", "norm", "q2", "k", "v", "m0", "m1", "m2")
UP = {"q0": 4, "q1": 4, "norm": 4, "q2": 4, "k": 4, "v": 3, "m0": 3, "m1": 3, "m2": 3}


def merged(base, low_turned, high):
    delta = lax.dot_general(
        low_turned, high, (((0,), (0,)), ((), ())), preferred_element_type=F32
    )
    return (base.astype(F32) + mix_rate * delta).astype(BF16)


def gather_kernel(
    wq, lq, hq, wk, lk, hk, wv, lv, hv, wm, lm, hm, nt, ns,
    q_all, k_all, v_all, m_all, n_out,
    wq_v, lq_v, hq_v, wk_v, lk_v, hk_v, wv_v, lv_v, hv_v, wm_v, lm_v, hm_v, nt_v, ns_v,
    n_all, n_wide,
    load_sem, pair_sem, side_sem, own_sem, send_sem, recv_sem, hand_sem, take_sem,
):
    zero = lax.axis_index("zero")
    col = lax.axis_index("cols")
    core = lax.rem(zero, 2)
    chip = lax.div(zero, 2)
    above = lax.rem(zero + 2, 16)
    below = lax.rem(zero + 14, 16)
    twin = zero + 1 - 2 * core

    barrier = pltpu.get_barrier_semaphore()
    for peer in (above, below, twin):
        pl.semaphore_signal(
            barrier, inc=1, device_id={"zero": peer}, device_id_type=MESH
        )
    for far in (1, 2, 3):
        pl.semaphore_signal(
            barrier,
            inc=1,
            device_id={"cols": lax.rem(col + far, 4)},
            device_id_type=MESH,
        )

    half = pl.ds(pl.multiple_of(384 * core, 128), 384)
    other_half = pl.ds(pl.multiple_of(384 * (1 - core), 128), 384)
    my_rows = pl.ds(pl.multiple_of(192 * core, 64), 192)
    loads = [
        pltpu.make_async_copy(src, dst, load_sem.at[i])
        for i, (src, dst) in enumerate(
            (
                (lq, lq_v),
                (hq, hq_v),
                (wq, wq_v),
                (nt, nt_v),
                (ns, ns_v),
                (lk, lk_v),
                (hk, hk_v),
                (wk, wk_v),
                (lv, lv_v),
                (hv, hv_v),
                (wv, wv_v),
                (hm, hm_v.at[core]),
                (wm.at[:, half], wm_v.at[my_rows]),
                (lm.at[:, half], lm_v),
            )
        )
    ]
    for load in loads:
        load.start()

    def place(name, origin):
        rows = 192 * (2 * origin + core)
        if name == "norm":
            return n_all.at[2 * origin + core]
        if name == "k":
            return k_all.at[pl.ds(pl.multiple_of(rows, 64), 192)]
        if name == "v":
            return v_all.at[pl.ds(pl.multiple_of(rows, 64), 192)]
        i = int(name[1])
        if name[0] == "q":
            return q_all.at[pl.ds(pl.multiple_of(rows + 64 * i, 64), 64)]
        return m_all.at[origin, pl.ds(pl.multiple_of(384 * core + 128 * i, 128), 128)]

    def ring_copy(name, way, step):
        i = PIECES.index(name)
        origin = lax.rem(chip + (8 - step if way == 0 else step), 8)
        piece = place(name, origin)
        return pltpu.make_async_remote_copy(
            src_ref=piece,
            dst_ref=piece,
            send_sem=send_sem.at[way, step, i],
            recv_sem=recv_sem.at[way, step, i],
            device_id={"zero": above if way == 0 else below},
            device_id_type=MESH,
        )

    def arrival(name, way, step):
        i = PIECES.index(name)
        origin = lax.rem(chip + (7 - step if way == 0 else step + 1), 8)
        piece = place(name, origin)
        return pltpu.make_async_remote_copy(
            src_ref=piece,
            dst_ref=piece,
            send_sem=send_sem.at[way, step, i],
            recv_sem=recv_sem.at[way, step, i],
            device_id={"zero": below if way == 0 else above},
            device_id_type=MESH,
        )

    def twin_place(name, origin):
        rows = 192 * (2 * origin + 1 - core)
        if name == "norm":
            return n_all.at[2 * origin + 1 - core]
        if name == "k":
            return k_all.at[pl.ds(pl.multiple_of(rows, 64), 192)]
        if name == "v":
            return v_all.at[pl.ds(pl.multiple_of(rows, 64), 192)]
        i = int(name[1])
        if name[0] == "q":
            return q_all.at[pl.ds(pl.multiple_of(rows + 64 * i, 64), 64)]
        return m_all.at[
            origin, pl.ds(pl.multiple_of(384 * (1 - core) + 128 * i, 128), 128)
        ]

    def hand(name, way, step):
        i = PIECES.index(name)
        if step < 0:
            origin = chip
        else:
            origin = lax.rem(chip + (7 - step if way == 0 else step + 1), 8)
        slot = step + 1
        mine = place(name, origin)
        return pltpu.make_async_remote_copy(
            src_ref=mine,
            dst_ref=mine,
            send_sem=hand_sem.at[way, slot, i],
            recv_sem=take_sem.at[way, slot, i],
            device_id={"zero": twin},
            device_id_type=MESH,
        )

    def take(name, way, step):
        i = PIECES.index(name)
        if step < 0:
            origin = chip
        else:
            origin = lax.rem(chip + (7 - step if way == 0 else step + 1), 8)
        slot = step + 1
        theirs = twin_place(name, origin)
        return pltpu.make_async_remote_copy(
            src_ref=theirs,
            dst_ref=theirs,
            send_sem=hand_sem.at[way, slot, i],
            recv_sem=take_sem.at[way, slot, i],
            device_id={"zero": twin},
            device_id_type=MESH,
        )

    def hops(name, way):
        return UP[name] if way == 0 else 7 - UP[name]

    sends, hands, takes = [], [], []

    def send(name, way, step):
        copy = ring_copy(name, way, step)
        copy.start()
        sends.append(copy)

    def give(name, way, step):
        copy = hand(name, way, step)
        copy.start()
        hands.append(copy)
        takes.append((name, way, step))

    def launch(name):
        send(name, 0, 0)
        send(name, 1, 0)
        give(name, 0, -1)

    for i in (0, 1, 2):
        loads[i].wait()
    own = 192 * zero
    q_all[pl.ds(pl.multiple_of(own, 64), 192), :] = merged(
        wq_v[...], lq_v[...], hq_v[...]
    )
    loads[3].wait()
    loads[4].wait()
    n_all[zero, col] = jnp.zeros((1, 128), F32)
    n_all[zero, col, :, 0:48] = nt_v[...] + ns_v[...]

    pl.semaphore_wait(barrier, 6)
    launch("q0")
    launch("q1")
    sides = []
    for far in (1, 2, 3):
        copy = pltpu.make_async_remote_copy(
            src_ref=n_all.at[zero, col],
            dst_ref=n_all.at[zero, col],
            send_sem=side_sem.at[0, far - 1],
            recv_sem=side_sem.at[1, far - 1],
            device_id={"cols": lax.rem(col + far, 4)},
            device_id_type=MESH,
        )
        copy.start()
        sides.append(copy)
    pair = [
        pltpu.make_async_remote_copy(
            src_ref=src,
            dst_ref=dst,
            send_sem=pair_sem.at[0, i],
            recv_sem=pair_sem.at[1, i],
            device_id={"zero": twin},
            device_id_type=MESH,
        )
        for i, (src, dst) in enumerate(
            ((wm.at[:, other_half], wm_v.at[my_rows]), (hm, hm_v.at[core]))
        )
    ]
    for copy in pair:
        copy.start()

    for i in (5, 6, 7):
        loads[i].wait()
    k_all[pl.ds(pl.multiple_of(own, 64), 192), :] = merged(
        wk_v[...], lk_v[...], hk_v[...]
    )
    for i in (8, 9, 10):
        loads[i].wait()
    v_all[pl.ds(pl.multiple_of(own, 64), 192), :] = merged(
        wv_v[...], lv_v[...], hv_v[...]
    )
    for far in (1, 2, 3):
        src = lax.rem(col + 4 - far, 4)
        pltpu.make_async_remote_copy(
            src_ref=n_all.at[zero, src],
            dst_ref=n_all.at[zero, src],
            send_sem=side_sem.at[0, far - 1],
            recv_sem=side_sem.at[1, far - 1],
            device_id={"cols": src},
            device_id_type=MESH,
        ).wait_recv()
    launch("norm")
    launch("q2")
    launch("k")
    launch("v")

    for i in (11, 12, 13):
        loads[i].wait()
    twin_rows = pl.ds(pl.multiple_of(192 * (1 - core), 64), 192)
    for i, dst in enumerate((wm_v.at[twin_rows], hm_v.at[1 - core])):
        pltpu.make_async_remote_copy(
            src_ref=dst,
            dst_ref=dst,
            send_sem=pair_sem.at[0, i],
            recv_sem=pair_sem.at[1, i],
            device_id={"zero": twin},
            device_id_type=MESH,
        ).wait_recv()
    row = lax.broadcasted_iota(jnp.int32, (192, 384), 0)
    lane = lax.broadcasted_iota(jnp.int32, (192, 384), 1)
    high = sum(
        jnp.dot(
            hm_v[c], (lane == row + 192 * c).astype(BF16), preferred_element_type=F32
        )
        for c in (0, 1)
    ).astype(BF16)
    for i in (0, 1, 2):
        lanes = slice(128 * i, 128 * i + 128)
        base = wm_v[:, lanes].astype(F32).T
        m_all[chip, pl.ds(pl.multiple_of(384 * core + 128 * i, 128), 128)] = merged(
            base, lm_v[:, lanes], high
        )
        launch(f"m{i}")
    for copy in sides + pair:
        copy.wait_send()

    def norm_out():
        for name, way, step in [t for t in takes if t[0] == "norm"]:
            take(name, way, step).wait_recv()
            takes.remove((name, way, step))
        at = lax.broadcasted_iota(jnp.int32, (1, 128), 1)
        for g in range(8):
            e = [n_all[2 * g + i // 4, i % 4] for i in range(8)]
            r = [pltpu.roll(e[i], (48 * i) % 128, 1) for i in range(8)]
            n_wide[3 * g : 3 * g + 1, :] = jnp.where(
                at < 48, r[0], jnp.where(at < 96, r[1], r[2])
            )
            n_wide[3 * g + 1 : 3 * g + 2, :] = jnp.where(
                at < 16,
                r[2],
                jnp.where(at < 64, r[3], jnp.where(at < 112, r[4], r[5])),
            )
            n_wide[3 * g + 2 : 3 * g + 3, :] = jnp.where(
                at < 32, r[5], jnp.where(at < 80, r[6], r[7])
            )
        n_out[...] = n_wide[...].astype(BF16)

    for step in range(4):
        todo = [
            [name for name in PIECES if step < hops(name, way)] for way in (0, 1)
        ]
        for n in range(max(map(len, todo))):
            if step == 3 and n == 4:
                norm_out()
                for copy in sends + hands:
                    copy.wait_send()
                del sends[:], hands[:]
            for way in (0, 1):
                if n < len(todo[way]):
                    name = todo[way][n]
                    arrival(name, way, step).wait_recv()
                    if step + 1 < hops(name, way):
                        send(name, way, step + 1)
                    give(name, way, step)
    for copy in sends + hands:
        copy.wait_send()
    for name, way, step in takes:
        take(name, way, step).wait_recv()


def store_kernel(q, k, v, m, n, q_out, k_out, v_out, m_out, n_out, sem):
    parts = [
        (q.at[pl.ds(768 * i, 768)], q_out.at[pl.ds(768 * i, 768)]) for i in range(4)
    ]
    parts += [(k, k_out), (v, v_out), (n, n_out)]
    parts += [(m.at[i], m_out.at[:, pl.ds(384 * i, 384)]) for i in range(8)]
    copies = [
        pltpu.make_async_copy(src, dst, sem.at[i]) for i, (src, dst) in enumerate(parts)
    ]
    for copy in copies:
        copy.start()
    for copy in copies:
        copy.wait()


def on_device(wq, lq, hq, wk, lk, hk, wv, lv, hv, wm, lm, hm, nt, ns):
    anywhere = pl.BlockSpec(memory_space=pltpu.HBM)
    onchip = pl.BlockSpec(memory_space=pltpu.VMEM)
    n = len(PIECES)
    held = pl.pallas_call(
        gather_kernel,
        out_shape=(
            pltpu.VMEM((3072, 768), BF16),
            pltpu.VMEM((3072, 256), BF16),
            pltpu.VMEM((3072, 256), BF16),
            pltpu.VMEM((8, 768, 384), BF16),
            pltpu.VMEM((24, 128), BF16),
        ),
        in_specs=[anywhere] * 14,
        out_specs=(onchip,) * 5,
        scratch_shapes=[
            pltpu.VMEM((192, 768), BF16),
            pltpu.VMEM((32, 192), BF16),
            pltpu.VMEM((32, 768), BF16),
            pltpu.VMEM((192, 256), BF16),
            pltpu.VMEM((32, 192), BF16),
            pltpu.VMEM((32, 256), BF16),
            pltpu.VMEM((192, 256), BF16),
            pltpu.VMEM((32, 192), BF16),
            pltpu.VMEM((32, 256), BF16),
            pltpu.VMEM((384, 384), BF16),
            pltpu.VMEM((32, 384), BF16),
            pltpu.VMEM((2, 32, 192), BF16),
            pltpu.VMEM((1, 48), F32),
            pltpu.VMEM((1, 48), F32),
            pltpu.VMEM((16, 4, 1, 128), F32),
            pltpu.VMEM((24, 128), F32),
            pltpu.SemaphoreType.DMA((14,)),
            pltpu.SemaphoreType.DMA((2, 2)),
            pltpu.SemaphoreType.DMA((2, 3)),
            pltpu.SemaphoreType.DMA,
            pltpu.SemaphoreType.DMA((2, 4, n)),
            pltpu.SemaphoreType.DMA((2, 4, n)),
            pltpu.SemaphoreType.DMA((2, 5, n)),
            pltpu.SemaphoreType.DMA((2, 5, n)),
        ],
        compiler_params=pltpu.CompilerParams(
            collective_id=0, has_side_effects=True, vmem_limit_bytes=54400000
        ),
        name="merge_and_gather",
    )(
        wq, lq.T, hq, wk, lk.T, hk, wv, lv.T, hv, wm.T, lm.T, hm,
        nt.reshape(1, 48), ns.reshape(1, 48),
    )
    q, k, v, m, norm = pl.pallas_call(
        store_kernel,
        out_shape=(
            jax.ShapeDtypeStruct((3072, 768), BF16),
            jax.ShapeDtypeStruct((3072, 256), BF16),
            jax.ShapeDtypeStruct((3072, 256), BF16),
            jax.ShapeDtypeStruct((768, 3072), BF16),
            jax.ShapeDtypeStruct((24, 128), BF16),
        ),
        in_specs=[onchip] * 5,
        out_specs=(anywhere,) * 5,
        scratch_shapes=[pltpu.SemaphoreType.DMA((15,))],
        compiler_params=pltpu.CompilerParams(vmem_limit_bytes=24 * 2**20),
        name="store",
    )(*held)
    return q, k, v, m, norm.reshape(3072)


def solution(mesh):
    placed = (
        P(("job", "zero"), "cols"),
        P(("job", "zero"), None),
        P("job", "cols"),
        P(("job", "zero"), "cols"),
        P(("job", "zero"), None),
        P("job", "cols"),
        P(("job", "zero"), "cols"),
        P(("job", "zero"), None),
        P("job", "cols"),
        P(("job", "cols"), "zero"),
        P(("job", "cols"), None),
        P("job", "zero"),
        P(("job", "zero", "cols")),
        P(("job", "zero", "cols")),
    )
    return jax.shard_map(
        on_device,
        mesh=mesh,
        in_specs=placed,
        out_specs=(
            P("job", "cols"),
            P("job", "cols"),
            P("job", "cols"),
            P(("job", "cols"), None),
            P("job"),
        ),
        check_vma=False,
    )
```

time: 120 us -> 79.6 us (0.66)
  Pallas kernels: 0 us -> 78.8 us
  waiting for transfers between devices: 57.3 us -> 0 us
  blocking collectives: 22 us -> 0 us
  local copies, waits for them, and re-layouts: 20 us -> 0 us
  between operations: 14.1 us -> 0.65 us
  matrix products: 4.81 us -> 0 us
    pallas_call x0 -> x2, Pallas kernels: none -> 78.8 us  [the longest x1 74.1 us: on_device(): pl.pallas_call(gather_kernel, out_shape=(pltpu.VMEM((3072, 768), BF16), p...]
    all_gather x1 -> x0, waiting for transfers between devices: 57.3 us -> none  [gather_turned(): whole = lax.all_gather(both, axis, axis=0, tiled=True)]
    all_to_all x1 -> x0, blocking collectives: 22 us -> none  [sent_to_all(): return lax.all_to_all(copies, axis, split_axis=0, concat_axis=0, tiled=True)]
    transpose x1 -> x0, local copies, waits for them, and re-layouts: 8.13 us -> none  [gather_turned(): jnp.moveaxis(b.reshape(-1, *t.shape[1:]), 0, dim)]
    unnamed x7 -> x0, local copies, waits for them, and re-layouts: 7.37 us -> none
    dot_general x4 -> x0, matrix products: 4.81 us -> none  [the longest x1 1.27 us: on_device(): jnp.dot(low_query, high_query, preferred_element_type=jnp.float32)]
    split x1 -> x0, local copies, waits for them, and re-layouts: 3.76 us -> none  [gather_turned(): jnp.split(whole, [sum(widths[:k]) for k in range(1, len(widths))], axis=1)]
  transfers between devices with their start and end apart: 1 -> 0, of which waited for: 1 -> 0; matrix products, arithmetic and copies ran while one was open for 1% -> 0% of each run, Pallas kernels for 0% -> 0%
where the time goes in v1:
time: 79.6 us; the launch traced here: 79.4 us
  Pallas kernels  78.8 us (99%)
    pallas_call x1, Pallas kernels, on_device(): pl.pallas_call(gather_kernel, out_shape=(pltpu.VMEM((3072, 768), BF16), p...  74.1 us
    pallas_call x1, Pallas kernels, on_device(): pl.pallas_call(store_kernel, out_shape=(jax.ShapeDtypeStruct((3072, 768),...  4.7 us

profile of v1, /device:TPU:1, one launch (start us, length us, event | category | flops | bytes accessed | tf_op | source)
XLA Modules:
  0.0 79.4 jit_solution(11637788429293602724)
XLA Ops:
  0.6 74.1 %merge_and_gather.1 = (bf16[3072,768]{1,0:T(8,128)(2,1)S(1)}, bf16[3072,256]{1,0:T(8,128)(2,1)S(1)}, bf16[3072,256]{1,0:T(8,128)(2,1)S(1)}, bf16[8,768,384]{2,1,0:T(8,128)(2,1)S(1)}, bf16[24,128]{1,0:T(8,128)(2,1)S(1)}) custom-call(bf16[192,768]{1,0:T(8,128)(2,1)} %wq.1, bf16[32,192]{1,0:T(8,128)(2,1)} %bitcast.10, bf16[32,768]{1,0:T(8,128)(2,1)} %hq.1, ...), custom_call_target="tpu_custom_call" | custom-call | tf_op jit(solution)/shard_map/merge_and_gather/pallas_call | solution.py:350
  74.7 4.7 %store.1 = (bf16[3072,768]{1,0:T(8,128)(2,1)}, bf16[3072,256]{1,0:T(8,128)(2,1)}, bf16[3072,256]{1,0:T(8,128)(2,1)}, bf16[768,3072]{1,0:T(8,128)(2,1)}, bf16[24,128]{1,0:T(8,128)(2,1)}) custom-call(bf16[3072,768]{1,0:T(8,128)(2,1)S(1)} %get-tuple-element.15.q, bf16[3072,256]{1,0:T(8,128)(2,1)S(1)} %get-tuple-element.16.k, ...), custom_call_target="tpu_custom_call" | custom-call | tf_op jit(solution)/shard_map/store/pallas_call | solution.py:395

commit v2 on v1

v2 whole, which is shorter than its diff:
```python
import functools

import jax
import jax.numpy as jnp
from jax import lax
from jax.experimental import pallas as pl
from jax.experimental.pallas import tpu as pltpu
from jax.sharding import PartitionSpec as P

mix_rate = 2.0
MESH = pl.DeviceIdType.MESH
BF16 = jnp.bfloat16
F32 = jnp.float32

PIECES = ("k", "v", "q", "norm", "m")
ORDER = (("k", "v", "q", "norm", "m"), ("k", "q", "norm", "m", "v"))
LAST = (("q", "norm", "v"), ("m", "k"))
UP = {"q": 4, "v": 4, "norm": 4, "k": 3, "m": 3}
KIND = {"q": 0, "k": 0, "v": 1, "m": 1, "norm": 2}
SIZE = {"q": 288, "k": 96, "v": 96, "m": 288, "norm": 2}


def by_arrival(orders):
    timed = []
    for way, order in enumerate(orders):
        at = 0
        for name in order:
            at += SIZE[name]
            timed.append((at, way, name))
    return [(name, way) for _, way, name in sorted(timed)]


def merged(base, low_turned, high):
    delta = lax.dot_general(
        low_turned, high, (((0,), (0,)), ((), ())), preferred_element_type=F32
    )
    return (base.astype(F32) + mix_rate * delta).astype(BF16)


def gather_kernel(
    wq, lq, hq, wk, lk, hk, wv, lv, hv, wm, lm, hm, nt, ns,
    q_all, k_all, v_all, m_all, n_out,
    wq_v, lq_v, hq_v, wk_v, lk_v, hk_v, wv_v, lv_v, hv_v, wm_v, lm_v, hm_v, nt_v, ns_v,
    n_all, n_wide,
    load_sem, pair_sem, side_sem, send_sem, recv_sem, hand_sem, take_sem,
):
    zero = lax.axis_index("zero")
    col = lax.axis_index("cols")
    core = lax.rem(zero, 2)
    chip = lax.div(zero, 2)
    above = lax.rem(zero + 2, 16)
    below = lax.rem(zero + 14, 16)
    twin = zero + 1 - 2 * core

    barrier = pltpu.get_barrier_semaphore()
    for peer in (above, below, twin):
        pl.semaphore_signal(
            barrier, inc=1, device_id={"zero": peer}, device_id_type=MESH
        )
    for far in (1, 2, 3):
        pl.semaphore_signal(
            barrier,
            inc=1,
            device_id={"cols": lax.rem(col + far, 4)},
            device_id_type=MESH,
        )

    half = pl.ds(pl.multiple_of(384 * core, 128), 384)
    other_half = pl.ds(pl.multiple_of(384 * (1 - core), 128), 384)
    my_rows = pl.ds(pl.multiple_of(192 * core, 64), 192)
    loads = [
        pltpu.make_async_copy(src, dst, load_sem.at[i])
        for i, (src, dst) in enumerate(
            (
                (lk, lk_v),
                (hk, hk_v),
                (wk, wk_v),
                (lv, lv_v),
                (hv, hv_v),
                (wv, wv_v),
                (lq, lq_v),
                (hq, hq_v),
                (wq, wq_v),
                (nt, nt_v),
                (ns, ns_v),
                (hm, hm_v.at[core]),
                (wm.at[:, half], wm_v.at[my_rows]),
                (lm.at[:, half], lm_v),
            )
        )
    ]
    for load in loads:
        load.start()

    def place(name, origin, of):
        if name == "norm":
            return n_all.at[2 * origin + of]
        if name == "m":
            return m_all.at[origin, pl.ds(pl.multiple_of(384 * of, 128), 384)]
        rows = pl.ds(pl.multiple_of(192 * (2 * origin + of), 64), 192)
        return {"q": q_all, "k": k_all, "v": v_all}[name].at[rows]

    arrivals = [
        (name, way, step)
        for way in (0, 1)
        for name in PIECES
        for step in range(UP[name] if way == 0 else 7 - UP[name])
    ]

    def arrived_from(way, step):
        return lax.rem(chip + (7 - step if way == 0 else step + 1), 8)

    def ring_copy(name, way, step):
        origin = lax.rem(chip + (8 - step if way == 0 else step), 8)
        piece = place(name, origin, core)
        return pltpu.make_async_remote_copy(
            src_ref=piece,
            dst_ref=piece,
            send_sem=send_sem.at[2 if name == "norm" else way],
            recv_sem=recv_sem.at[arrivals.index((name, way, step))],
            device_id={"zero": above if way == 0 else below},
            device_id_type=MESH,
        )

    def arrival(name, way, step):
        piece = place(name, arrived_from(way, step), core)
        return pltpu.make_async_remote_copy(
            src_ref=piece,
            dst_ref=piece,
            send_sem=send_sem.at[2 if name == "norm" else way],
            recv_sem=recv_sem.at[arrivals.index((name, way, step))],
            device_id={"zero": below if way == 0 else above},
            device_id_type=MESH,
        )

    def give(name, way, step):
        origin = chip if step < 0 else arrived_from(way, step)
        piece = place(name, origin, core)
        pltpu.make_async_remote_copy(
            src_ref=piece,
            dst_ref=piece,
            send_sem=hand_sem.at[KIND[name]],
            recv_sem=take_sem.at[KIND[name]],
            device_id={"zero": twin},
            device_id_type=MESH,
        ).start()

    def send(name, way, step):
        ring_copy(name, way, step).start()

    def drain(sem, *refs):
        for ref in refs:
            pltpu.make_async_copy(ref, ref, sem).wait()

    own = pl.ds(pl.multiple_of(192 * zero, 64), 192)
    for i in (0, 1, 2):
        loads[i].wait()
    k_all[own, :] = merged(wk_v[...], lk_v[...], hk_v[...])
    pl.semaphore_wait(barrier, 6)
    send("k", 0, 0)
    send("k", 1, 0)
    for i in (3, 4, 5):
        loads[i].wait()
    v_all[own, :] = merged(wv_v[...], lv_v[...], hv_v[...])
    send("v", 0, 0)
    for i in (6, 7, 8):
        loads[i].wait()
    q_all[own, :] = merged(wq_v[...], lq_v[...], hq_v[...])
    send("q", 0, 0)
    send("q", 1, 0)

    loads[9].wait()
    loads[10].wait()
    n_all[zero, col] = jnp.zeros((1, 128), F32)
    n_all[zero, col, :, 0:48] = nt_v[...] + ns_v[...]
    pair = [
        pltpu.make_async_remote_copy(
            src_ref=src,
            dst_ref=dst,
            send_sem=pair_sem.at[0, i],
            recv_sem=pair_sem.at[1, i],
            device_id={"zero": twin},
            device_id_type=MESH,
        )
        for i, (src, dst) in enumerate(
            ((wm.at[:, other_half], wm_v.at[my_rows]), (hm, hm_v.at[core]))
        )
    ]
    for copy in pair:
        copy.start()
    sides = []
    for far in (1, 2, 3):
        copy = pltpu.make_async_remote_copy(
            src_ref=n_all.at[zero, col],
            dst_ref=n_all.at[zero, col],
            send_sem=side_sem.at[0, far - 1],
            recv_sem=side_sem.at[1, far - 1],
            device_id={"cols": lax.rem(col + far, 4)},
            device_id_type=MESH,
        )
        copy.start()
        sides.append(copy)
    for name in ("k", "v", "q"):
        give(name, 0, -1)

    for i in (11, 12, 13):
        loads[i].wait()
    twin_rows = pl.ds(pl.multiple_of(192 * (1 - core), 64), 192)
    for i, dst in enumerate((wm_v.at[twin_rows], hm_v.at[1 - core])):
        pltpu.make_async_remote_copy(
            src_ref=dst,
            dst_ref=dst,
            send_sem=pair_sem.at[0, i],
            recv_sem=pair_sem.at[1, i],
            device_id={"zero": twin},
            device_id_type=MESH,
        ).wait_recv()
    row = lax.broadcasted_iota(jnp.int32, (192, 384), 0)
    lane = lax.broadcasted_iota(jnp.int32, (192, 384), 1)
    high = sum(
        jnp.dot(
            hm_v[c], (lane == row + 192 * c).astype(BF16), preferred_element_type=F32
        )
        for c in (0, 1)
    ).astype(BF16)
    for i in (0, 1, 2):
        lanes = slice(128 * i, 128 * i + 128)
        base = wm_v[:, lanes].astype(F32).T
        m_all[chip, pl.ds(pl.multiple_of(384 * core + 128 * i, 128), 128)] = merged(
            base, lm_v[:, lanes], high
        )
    for far in (1, 2, 3):
        src = lax.rem(col + 4 - far, 4)
        pltpu.make_async_remote_copy(
            src_ref=n_all.at[zero, src],
            dst_ref=n_all.at[zero, src],
            send_sem=side_sem.at[0, far - 1],
            recv_sem=side_sem.at[1, far - 1],
            device_id={"cols": src},
            device_id_type=MESH,
        ).wait_recv()
    send("norm", 0, 0)
    send("norm", 1, 0)
    send("m", 0, 0)
    send("m", 1, 0)
    send("v", 1, 0)
    give("norm", 0, -1)
    give("m", 0, -1)
    for copy in sides + pair:
        copy.wait_send()

    def norm_out():
        drain(take_sem.at[2], n_all.at[0:8])
        at = lax.broadcasted_iota(jnp.int32, (1, 128), 1)
        for g in range(8):
            e = [n_all[2 * g + i // 4, i % 4] for i in range(8)]
            r = [pltpu.roll(e[i], (48 * i) % 128, 1) for i in range(8)]
            n_wide[3 * g : 3 * g + 1, :] = jnp.where(
                at < 48, r[0], jnp.where(at < 96, r[1], r[2])
            )
            n_wide[3 * g + 1 : 3 * g + 2, :] = jnp.where(
                at < 16,
                r[2],
                jnp.where(at < 64, r[3], jnp.where(at < 112, r[4], r[5])),
            )
            n_wide[3 * g + 2 : 3 * g + 3, :] = jnp.where(
                at < 32, r[5], jnp.where(at < 80, r[6], r[7])
            )
        n_out[...] = n_wide[...].astype(BF16)

    for step in range(3):
        for name, way in by_arrival(ORDER):
            arrival(name, way, step).wait_recv()
            if step < 2:
                send(name, way, step + 1)
            elif name == LAST[way][-2]:
                send(name, way, 3)
                send(LAST[way][-1], way, 3)
            elif name in LAST[way][:-2]:
                send(name, way, 3)
            give(name, way, step)
    last = by_arrival(LAST)
    for name, way in last[:-2]:
        arrival(name, way, 3).wait_recv()
        give(name, way, 3)
    norm_out()
    for name, way in last[-2:]:
        arrival(name, way, 3).wait_recv()
        give(name, way, 3)
    for way in (0, 1):
        drain(send_sem.at[way], q_all.at[0:1792])
    drain(send_sem.at[2], n_all.at[0:7])
    drain(hand_sem.at[2], n_all.at[0:8])
    for kind in (0, 1):
        drain(hand_sem.at[kind], q_all.at[0:2048])
        drain(take_sem.at[kind], q_all.at[0:2048])


def store_kernel(q, k, v, m, n, q_out, k_out, v_out, m_out, n_out, sem):
    parts = [
        (q.at[pl.ds(768 * i, 768)], q_out.at[pl.ds(768 * i, 768)], 0) for i in range(4)
    ]
    parts += [(m.at[i], m_out.at[:, pl.ds(384 * i, 384)], 1) for i in range(8)]
    parts += [(k, k_out, 2), (v, v_out, 3), (n, n_out, 4)]
    for src, dst, i in parts:
        pltpu.make_async_copy(src, dst, sem.at[i]).start()
    for i, (src, dst) in enumerate(
        ((q, q_out), (m_out, m_out), (k, k_out), (v, v_out), (n, n_out))
    ):
        pltpu.make_async_copy(src, dst, sem.at[i]).wait()


def on_device(wq, lq, hq, wk, lk, hk, wv, lv, hv, wm, lm, hm, nt, ns):
    anywhere = pl.BlockSpec(memory_space=pltpu.HBM)
    onchip = pl.BlockSpec(memory_space=pltpu.VMEM)
    held = pl.pallas_call(
        gather_kernel,
        out_shape=(
            pltpu.VMEM((3072, 768), BF16),
            pltpu.VMEM((3072, 256), BF16),
            pltpu.VMEM((3072, 256), BF16),
            pltpu.VMEM((8, 768, 384), BF16),
            pltpu.VMEM((24, 128), BF16),
        ),
        in_specs=[anywhere] * 14,
        out_specs=(onchip,) * 5,
        scratch_shapes=[
            pltpu.VMEM((192, 768), BF16),
            pltpu.VMEM((32, 192), BF16),
            pltpu.VMEM((32, 768), BF16),
            pltpu.VMEM((192, 256), BF16),
            pltpu.VMEM((32, 192), BF16),
            pltpu.VMEM((32, 256), BF16),
            pltpu.VMEM((192, 256), BF16),
            pltpu.VMEM((32, 192), BF16),
            pltpu.VMEM((32, 256), BF16),
            pltpu.VMEM((384, 384), BF16),
            pltpu.VMEM((32, 384), BF16),
            pltpu.VMEM((2, 32, 192), BF16),
            pltpu.VMEM((1, 48), F32),
            pltpu.VMEM((1, 48), F32),
            pltpu.VMEM((16, 4, 1, 128), F32),
            pltpu.VMEM((24, 128), F32),
            pltpu.SemaphoreType.DMA((14,)),
            pltpu.SemaphoreType.DMA((2, 2)),
            pltpu.SemaphoreType.DMA((2, 3)),
            pltpu.SemaphoreType.DMA((3,)),
            pltpu.SemaphoreType.DMA((7 * len(PIECES),)),
            pltpu.SemaphoreType.DMA((3,)),
            pltpu.SemaphoreType.DMA((3,)),
        ],
        compiler_params=pltpu.CompilerParams(
            collective_id=0, has_side_effects=True, vmem_limit_bytes=54400000
        ),
        name="merge_and_gather",
    )(
        wq, lq.T, hq, wk, lk.T, hk, wv, lv.T, hv, wm.T, lm.T, hm,
        nt.reshape(1, 48), ns.reshape(1, 48),
    )
    q, k, v, m, norm = pl.pallas_call(
        store_kernel,
        out_shape=(
            jax.ShapeDtypeStruct((3072, 768), BF16),
            jax.ShapeDtypeStruct((3072, 256), BF16),
            jax.ShapeDtypeStruct((3072, 256), BF16),
            jax.ShapeDtypeStruct((768, 3072), BF16),
            jax.ShapeDtypeStruct((24, 128), BF16),
        ),
        in_specs=[onchip] * 5,
        out_specs=(anywhere,) * 5,
        scratch_shapes=[pltpu.SemaphoreType.DMA((5,))],
        compiler_params=pltpu.CompilerParams(vmem_limit_bytes=24 * 2**20),
        name="store",
    )(*held)
    return q, k, v, m, norm.reshape(3072)


def solution(mesh):
    placed = (
        P(("job", "zero"), "cols"),
        P(("job", "zero"), None),
        P("job", "cols"),
        P(("job", "zero"), "cols"),
        P(("job", "zero"), None),
        P("job", "cols"),
        P(("job", "zero"), "cols"),
        P(("job", "zero"), None),
        P("job", "cols"),
        P(("job", "cols"), "zero"),
        P(("job", "cols"), None),
        P("job", "zero"),
        P(("job", "zero", "cols")),
        P(("job", "zero", "cols")),
    )
    return jax.shard_map(
        on_device,
        mesh=mesh,
        in_specs=placed,
        out_specs=(
            P("job", "cols"),
            P("job", "cols"),
            P("job", "cols"),
            P(("job", "cols"), None),
            P("job"),
        ),
        check_vma=False,
    )
```

time: 79.6 us -> 77.8 us (0.977)
  Pallas kernels: 78.8 us -> 77 us
    pallas_call x1, Pallas kernels: 74.1 us -> 72.4 us  [on_device(): pl.pallas_call(gather_kernel, out_shape=(pltpu.VMEM((3072, 768), BF16), p...]
where the time goes in v2:
time: 77.8 us; the launch traced here: 77.7 us
  Pallas kernels  77 us (99%)
    pallas_call x1, Pallas kernels, on_device(): pl.pallas_call(gather_kernel, out_shape=(pltpu.VMEM((3072, 768), BF16), p...  72.4 us
    pallas_call x1, Pallas kernels, on_device(): pl.pallas_call(store_kernel, out_shape=(jax.ShapeDtypeStruct((3072, 768),...  4.64 us

profile of v2, /device:TPU:1, one launch (start us, length us, event | category | flops | bytes accessed | tf_op | source)
XLA Modules:
  0.0 77.7 jit_solution(8206749030500912234)
XLA Ops:
  0.6 72.4 %merge_and_gather.1 = (bf16[3072,768]{1,0:T(8,128)(2,1)S(1)}, bf16[3072,256]{1,0:T(8,128)(2,1)S(1)}, bf16[3072,256]{1,0:T(8,128)(2,1)S(1)}, bf16[8,768,384]{2,1,0:T(8,128)(2,1)S(1)}, bf16[24,128]{1,0:T(8,128)(2,1)S(1)}) custom-call(bf16[192,768]{1,0:T(8,128)(2,1)} %wq.1, bf16[32,192]{1,0:T(8,128)(2,1)} %bitcast.10, bf16[32,768]{1,0:T(8,128)(2,1)} %hq.1, ...), custom_call_target="tpu_custom_call" | custom-call | tf_op jit(solution)/shard_map/merge_and_gather/pallas_call | solution.py:316
  73.0 4.6 %store.1 = (bf16[3072,768]{1,0:T(8,128)(2,1)}, bf16[3072,256]{1,0:T(8,128)(2,1)}, bf16[3072,256]{1,0:T(8,128)(2,1)}, bf16[768,3072]{1,0:T(8,128)(2,1)}, bf16[24,128]{1,0:T(8,128)(2,1)}) custom-call(bf16[3072,768]{1,0:T(8,128)(2,1)S(1)} %get-tuple-element.15.q, bf16[3072,256]{1,0:T(8,128)(2,1)S(1)} %get-tuple-element.16.k, ...), custom_call_target="tpu_custom_call" | custom-call | tf_op jit(solution)/shard_map/store/pallas_call | solution.py:360

commit v3 on v2

--- a/solution.py
+++ b/solution.py
@@ -12,12 +12,12 @@
 BF16 = jnp.bfloat16
 F32 = jnp.float32
 
-PIECES = ("k", "v", "q", "norm", "m")
-ORDER = (("k", "v", "q", "norm", "m"), ("k", "q", "norm", "m", "v"))
-LAST = (("q", "norm", "v"), ("m", "k"))
-UP = {"q": 4, "v": 4, "norm": 4, "k": 3, "m": 3}
-KIND = {"q": 0, "k": 0, "v": 1, "m": 1, "norm": 2}
-SIZE = {"q": 288, "k": 96, "v": 96, "m": 288, "norm": 2}
+PIECES = ("k", "v", "q", "m")
+ORDER = (("k", "v", "q", "m"), ("k", "q", "m", "v"))
+LAST = (("q", "v"), ("m", "k"))
+UP = {"q": 4, "v": 4, "k": 3, "m": 3}
+KIND = {"q": 0, "k": 0, "v": 1, "m": 1}
+SIZE = {"q": 288, "k": 96, "v": 96, "m": 288}
 
 
 def by_arrival(orders):
@@ -42,7 +42,7 @@
     q_all, k_all, v_all, m_all, n_out,
     wq_v, lq_v, hq_v, wk_v, lk_v, hk_v, wv_v, lv_v, hv_v, wm_v, lm_v, hm_v, nt_v, ns_v,
     n_all, n_wide,
-    load_sem, pair_sem, side_sem, send_sem, recv_sem, hand_sem, take_sem,
+    load_sem, pair_sem, send_sem, recv_sem, hand_sem, take_sem, norm_sem,
 ):
     zero = lax.axis_index("zero")
     col = lax.axis_index("cols")
@@ -57,13 +57,21 @@
         pl.semaphore_signal(
             barrier, inc=1, device_id={"zero": peer}, device_id_type=MESH
         )
-    for far in (1, 2, 3):
-        pl.semaphore_signal(
-            barrier,
-            inc=1,
-            device_id={"cols": lax.rem(col + far, 4)},
-            device_id_type=MESH,
-        )
+    is_root = zero == 0
+
+    @pl.when(is_root)
+    def _():
+        for other in range(1, 16):
+            pl.semaphore_signal(
+                barrier, inc=1, device_id={"zero": other}, device_id_type=MESH
+            )
+        for far in (1, 2, 3):
+            pl.semaphore_signal(
+                barrier,
+                inc=1,
+                device_id={"cols": lax.rem(col + far, 4)},
+                device_id_type=MESH,
+            )
 
     half = pl.ds(pl.multiple_of(384 * core, 128), 384)
     other_half = pl.ds(pl.multiple_of(384 * (1 - core), 128), 384)
@@ -75,14 +83,14 @@
                 (lk, lk_v),
                 (hk, hk_v),
                 (wk, wk_v),
+                (nt, nt_v),
+                (ns, ns_v),
                 (lv, lv_v),
                 (hv, hv_v),
                 (wv, wv_v),
                 (lq, lq_v),
                 (hq, hq_v),
                 (wq, wq_v),
-                (nt, nt_v),
-                (ns, ns_v),
                 (hm, hm_v.at[core]),
                 (wm.at[:, half], wm_v.at[my_rows]),
                 (lm.at[:, half], lm_v),
@@ -93,8 +101,6 @@
         load.start()
 
     def place(name, origin, of):
-        if name == "norm":
-            return n_all.at[2 * origin + of]
         if name == "m":
             return m_all.at[origin, pl.ds(pl.multiple_of(384 * of, 128), 384)]
         rows = pl.ds(pl.multiple_of(192 * (2 * origin + of), 64), 192)
@@ -116,7 +122,7 @@
         return pltpu.make_async_remote_copy(
             src_ref=piece,
             dst_ref=piece,
-            send_sem=send_sem.at[2 if name == "norm" else way],
+            send_sem=send_sem.at[way],
             recv_sem=recv_sem.at[arrivals.index((name, way, step))],
             device_id={"zero": above if way == 0 else below},
             device_id_type=MESH,
@@ -127,7 +133,7 @@
         return pltpu.make_async_remote_copy(
             src_ref=piece,
             dst_ref=piece,
-            send_sem=send_sem.at[2 if name == "norm" else way],
+            send_sem=send_sem.at[way],
             recv_sem=recv_sem.at[arrivals.index((name, way, step))],
             device_id={"zero": below if way == 0 else above},
             device_id_type=MESH,
@@ -156,23 +162,35 @@
     for i in (0, 1, 2):
         loads[i].wait()
     k_all[own, :] = merged(wk_v[...], lk_v[...], hk_v[...])
-    pl.semaphore_wait(barrier, 6)
+    loads[3].wait()
+    loads[4].wait()
+    n_all[col, zero] = jnp.zeros((1, 128), F32)
+    n_all[col, zero, :, 0:48] = nt_v[...] + ns_v[...]
+    row_copy = pltpu.make_async_remote_copy(
+        src_ref=n_all.at[col, zero],
+        dst_ref=n_all.at[col, zero],
+        send_sem=norm_sem.at[0],
+        recv_sem=norm_sem.at[1],
+        device_id={"zero": 0},
+        device_id_type=MESH,
+    )
+    pl.semaphore_wait(barrier, jnp.where(is_root, 6, 4))
     send("k", 0, 0)
     send("k", 1, 0)
-    for i in (3, 4, 5):
+    for i in (5, 6, 7):
         loads[i].wait()
     v_all[own, :] = merged(wv_v[...], lv_v[...], hv_v[...])
     send("v", 0, 0)
-    for i in (6, 7, 8):
+    for i in (8, 9, 10):
         loads[i].wait()
     q_all[own, :] = merged(wq_v[...], lq_v[...], hq_v[...])
     send("q", 0, 0)
     send("q", 1, 0)
 
-    loads[9].wait()
-    loads[10].wait()
-    n_all[zero, col] = jnp.zeros((1, 128), F32)
-    n_all[zero, col, :, 0:48] = nt_v[...] + ns_v[...]
+    @pl.when(jnp.logical_not(is_root))
+    def _():
+        row_copy.start()
+
     pair = [
         pltpu.make_async_remote_copy(
             src_ref=src,
@@ -188,18 +206,6 @@
     ]
     for copy in pair:
         copy.start()
-    sides = []
-    for far in (1, 2, 3):
-        copy = pltpu.make_async_remote_copy(
-            src_ref=n_all.at[zero, col],
-            dst_ref=n_all.at[zero, col],
-            send_sem=side_sem.at[0, far - 1],
-            recv_sem=side_sem.at[1, far - 1],
-            device_id={"cols": lax.rem(col + far, 4)},
-            device_id_type=MESH,
-        )
-        copy.start()
-        sides.append(copy)
     for name in ("k", "v", "q"):
         give(name, 0, -1)
 
@@ -229,31 +235,30 @@
         m_all[chip, pl.ds(pl.multiple_of(384 * core + 128 * i, 128), 128)] = merged(
             base, lm_v[:, lanes], high
         )
-    for far in (1, 2, 3):
-        src = lax.rem(col + 4 - far, 4)
-        pltpu.make_async_remote_copy(
-            src_ref=n_all.at[zero, src],
-            dst_ref=n_all.at[zero, src],
-            send_sem=side_sem.at[0, far - 1],
-            recv_sem=side_sem.at[1, far - 1],
-            device_id={"cols": src},
-            device_id_type=MESH,
-        ).wait_recv()
-    send("norm", 0, 0)
-    send("norm", 1, 0)
     send("m", 0, 0)
     send("m", 1, 0)
     send("v", 1, 0)
-    give("norm", 0, -1)
     give("m", 0, -1)
-    for copy in sides + pair:
+    for copy in pair:
         copy.wait_send()
 
-    def norm_out():
-        drain(take_sem.at[2], n_all.at[0:8])
+    def meet_columns():
+        drain(norm_sem.at[1], n_all.at[0, 0:15])
+        for far in (1, 2, 3):
+            pltpu.make_async_remote_copy(
+                src_ref=n_all.at[col],
+                dst_ref=n_all.at[col],
+                send_sem=norm_sem.at[2],
+                recv_sem=norm_sem.at[3],
+                device_id={"cols": lax.rem(col + far, 4)},
+                device_id_type=MESH,
+            ).start()
+
+    def assemble():
+        drain(norm_sem.at[3], n_all.at[0:3])
         at = lax.broadcasted_iota(jnp.int32, (1, 128), 1)
         for g in range(8):
-            e = [n_all[2 * g + i // 4, i % 4] for i in range(8)]
+            e = [n_all[i % 4, 2 * g + i // 4] for i in range(8)]
             r = [pltpu.roll(e[i], (48 * i) % 128, 1) for i in range(8)]
             n_wide[3 * g : 3 * g + 1, :] = jnp.where(
                 at < 48, r[0], jnp.where(at < 96, r[1], r[2])
@@ -268,29 +273,60 @@
             )
         n_out[...] = n_wide[...].astype(BF16)
 
+    def norm_copy(to):
+        return pltpu.make_async_remote_copy(
+            src_ref=n_out,
+            dst_ref=n_out,
+            send_sem=norm_sem.at[4],
+            recv_sem=norm_sem.at[5],
+            device_id={"zero": to},
+            device_id_type=MESH,
+        )
+
+    def spread():
+        for to in (1, 2, 14, 4, 12, 6, 10, 8):
+            norm_copy(to).start()
+
+    at_root = {2: meet_columns, 4: assemble, 6: spread}
+
     for step in range(3):
-        for name, way in by_arrival(ORDER):
+        for n, (name, way) in enumerate(by_arrival(ORDER)):
             arrival(name, way, step).wait_recv()
             if step < 2:
                 send(name, way, step + 1)
             elif name == LAST[way][-2]:
                 send(name, way, 3)
                 send(LAST[way][-1], way, 3)
-            elif name in LAST[way][:-2]:
+            elif name == LAST[way][0]:
                 send(name, way, 3)
             give(name, way, step)
+            if step == 0 and n in at_root:
+                pl.when(is_root)(at_root[n])
     last = by_arrival(LAST)
     for name, way in last[:-2]:
         arrival(name, way, 3).wait_recv()
         give(name, way, 3)
-    norm_out()
+
+    @pl.when(is_root)
+    def _():
+        drain(norm_sem.at[2], n_all.at[0:3])
+        drain(norm_sem.at[4], q_all.at[0:32])
+
+    @pl.when(jnp.logical_not(is_root))
+    def _():
+        row_copy.wait_send()
+        norm_copy(twin).wait_recv()
+
+    @pl.when(jnp.logical_and(core == 0, jnp.logical_not(is_root)))
+    def _():
+        norm_copy(twin).start()
+        norm_copy(twin).wait_send()
+
     for name, way in last[-2:]:
         arrival(name, way, 3).wait_recv()
         give(name, way, 3)
     for way in (0, 1):
         drain(send_sem.at[way], q_all.at[0:1792])
-    drain(send_sem.at[2], n_all.at[0:7])
-    drain(hand_sem.at[2], n_all.at[0:8])
     for kind in (0, 1):
         drain(hand_sem.at[kind], q_all.at[0:2048])
         drain(take_sem.at[kind], q_all.at[0:2048])
@@ -339,15 +375,15 @@
             pltpu.VMEM((2, 32, 192), BF16),
             pltpu.VMEM((1, 48), F32),
             pltpu.VMEM((1, 48), F32),
-            pltpu.VMEM((16, 4, 1, 128), F32),
+            pltpu.VMEM((4, 16, 1, 128), F32),
             pltpu.VMEM((24, 128), F32),
             pltpu.SemaphoreType.DMA((14,)),
             pltpu.SemaphoreType.DMA((2, 2)),
-            pltpu.SemaphoreType.DMA((2, 3)),
-            pltpu.SemaphoreType.DMA((3,)),
+            pltpu.SemaphoreType.DMA((2,)),
             pltpu.SemaphoreType.DMA((7 * len(PIECES),)),
-            pltpu.SemaphoreType.DMA((3,)),
-            pltpu.SemaphoreType.DMA((3,)),
+            pltpu.SemaphoreType.DMA((2,)),
+            pltpu.SemaphoreType.DMA((2,)),
+            pltpu.SemaphoreType.DMA((6,)),
         ],
         compiler_params=pltpu.CompilerParams(
             collective_id=0, has_side_effects=True, vmem_limit_bytes=54400000

time: 77.8 us -> 75.3 us (0.968)
  Pallas kernels: 77 us -> 74.5 us
    pallas_call x1, Pallas kernels: 72.4 us -> 69.9 us  [on_device(): pl.pallas_call(gather_kernel, out_shape=(pltpu.VMEM((3072, 768), BF16), p...]
where the time goes in v3:
time: 75.3 us; the launch traced here: 75.1 us
  Pallas kernels  74.5 us (99%)
    pallas_call x1, Pallas kernels, on_device(): pl.pallas_call(gather_kernel, out_shape=(pltpu.VMEM((3072, 768), BF16), p...  69.9 us
    pallas_call x1, Pallas kernels, on_device(): pl.pallas_call(store_kernel, out_shape=(jax.ShapeDtypeStruct((3072, 768),...  4.64 us

profile of v3, /device:TPU:1, one launch (start us, length us, event | category | flops | bytes accessed | tf_op | source)
XLA Modules:
  0.0 75.1 jit_solution(3523671857803061049)
XLA Ops:
  0.6 69.9 %merge_and_gather.1 = (bf16[3072,768]{1,0:T(8,128)(2,1)S(1)}, bf16[3072,256]{1,0:T(8,128)(2,1)S(1)}, bf16[3072,256]{1,0:T(8,128)(2,1)S(1)}, bf16[8,768,384]{2,1,0:T(8,128)(2,1)S(1)}, bf16[24,128]{1,0:T(8,128)(2,1)S(1)}) custom-call(bf16[192,768]{1,0:T(8,128)(2,1)} %wq.1, bf16[32,192]{1,0:T(8,128)(2,1)} %bitcast.10, bf16[32,768]{1,0:T(8,128)(2,1)} %hq.1, ...), custom_call_target="tpu_custom_call" | custom-call | tf_op jit(solution)/shard_map/merge_and_gather/pallas_call | solution.py:352
  70.5 4.6 %store.1 = (bf16[3072,768]{1,0:T(8,128)(2,1)}, bf16[3072,256]{1,0:T(8,128)(2,1)}, bf16[3072,256]{1,0:T(8,128)(2,1)}, bf16[768,3072]{1,0:T(8,128)(2,1)}, bf16[24,128]{1,0:T(8,128)(2,1)}) custom-call(bf16[3072,768]{1,0:T(8,128)(2,1)S(1)} %get-tuple-element.15.q, bf16[3072,256]{1,0:T(8,128)(2,1)S(1)} %get-tuple-element.16.k, ...), custom_call_target="tpu_custom_call" | custom-call | tf_op jit(solution)/shard_map/store/pallas_call | solution.py:396

commit v4 on v3

--- a/solution.py
+++ b/solution.py
@@ -42,7 +42,7 @@
     q_all, k_all, v_all, m_all, n_out,
     wq_v, lq_v, hq_v, wk_v, lk_v, hk_v, wv_v, lv_v, hv_v, wm_v, lm_v, hm_v, nt_v, ns_v,
     n_all, n_wide,
-    load_sem, pair_sem, send_sem, recv_sem, hand_sem, take_sem, norm_sem,
+    load_sem, pair_sem, send_sem, recv_sem, hand_sem, take_sem, norm_sem, ready_sem,
 ):
     zero = lax.axis_index("zero")
     col = lax.axis_index("cols")
@@ -53,18 +53,22 @@
     twin = zero + 1 - 2 * core
 
     barrier = pltpu.get_barrier_semaphore()
-    for peer in (above, below, twin):
+
+    def greet(peer):
         pl.semaphore_signal(
             barrier, inc=1, device_id={"zero": peer}, device_id_type=MESH
         )
+
+    greet(twin)
+    pl.when(chip != 7)(lambda: greet(above))
+    pl.when(jnp.logical_or(chip == 0, chip >= 5))(lambda: greet(below))
+
     is_root = zero == 0
 
     @pl.when(is_root)
     def _():
         for other in range(1, 16):
-            pl.semaphore_signal(
-                barrier, inc=1, device_id={"zero": other}, device_id_type=MESH
-            )
+            greet(other)
         for far in (1, 2, 3):
             pl.semaphore_signal(
                 barrier,
@@ -111,7 +115,7 @@
         for way in (0, 1)
         for name in PIECES
         for step in range(UP[name] if way == 0 else 7 - UP[name])
-    ]
+    ] + [("v", 1, 3)]
 
     def arrived_from(way, step):
         return lax.rem(chip + (7 - step if way == 0 else step + 1), 8)
@@ -174,23 +178,6 @@
         device_id={"zero": 0},
         device_id_type=MESH,
     )
-    pl.semaphore_wait(barrier, jnp.where(is_root, 6, 4))
-    send("k", 0, 0)
-    send("k", 1, 0)
-    for i in (5, 6, 7):
-        loads[i].wait()
-    v_all[own, :] = merged(wv_v[...], lv_v[...], hv_v[...])
-    send("v", 0, 0)
-    for i in (8, 9, 10):
-        loads[i].wait()
-    q_all[own, :] = merged(wq_v[...], lq_v[...], hq_v[...])
-    send("q", 0, 0)
-    send("q", 1, 0)
-
-    @pl.when(jnp.logical_not(is_root))
-    def _():
-        row_copy.start()
-
     pair = [
         pltpu.make_async_remote_copy(
             src_ref=src,
@@ -204,8 +191,66 @@
             ((wm.at[:, other_half], wm_v.at[my_rows]), (hm, hm_v.at[core]))
         )
     ]
+    pl.semaphore_wait(
+        barrier,
+        1
+        + jnp.where(chip == 0, 0, 1)
+        + jnp.where(chip >= 4, 1, 0)
+        + jnp.where(is_root, 3, 1),
+    )
+
+    def ready(peer, i):
+        pl.semaphore_signal(
+            ready_sem.at[i], inc=1, device_id={"zero": peer}, device_id_type=MESH
+        )
+
+    pl.when(jnp.logical_and(chip >= 1, chip <= 4))(lambda: ready(below, 0))
+    pl.when(chip == 7)(lambda: ready(above, 1))
+    first = chip == 0
+    early = jnp.logical_and(chip >= 1, chip <= 3)
+    late = chip >= 4
+
+    @pl.when(first)
+    def _():
+        pl.semaphore_wait(ready_sem.at[0], 1)
+        send("k", 0, 0)
+
+    @pl.when(jnp.logical_not(first))
+    def _():
+        send("k", 1, 0)
+
+    pl.when(late)(lambda: send("k", 0, 0))
     for copy in pair:
         copy.start()
+    for i in (5, 6, 7):
+        loads[i].wait()
+    v_all[own, :] = merged(wv_v[...], lv_v[...], hv_v[...])
+    for i in (8, 9, 10):
+        loads[i].wait()
+    q_all[own, :] = merged(wq_v[...], lq_v[...], hq_v[...])
+
+    @pl.when(jnp.logical_not(first))
+    def _():
+        send("q", 1, 0)
+
+    @pl.when(early)
+    def _():
+        pl.semaphore_wait(ready_sem.at[0], 1)
+        send("k", 0, 0)
+
+    send("v", 0, 0)
+    send("q", 0, 0)
+
+    @pl.when(first)
+    def _():
+        pl.semaphore_wait(ready_sem.at[1], 1)
+        send("k", 1, 0)
+        send("q", 1, 0)
+
+    @pl.when(jnp.logical_not(is_root))
+    def _():
+        row_copy.start()
+
     for name in ("k", "v", "q"):
         give(name, 0, -1)
 
@@ -294,11 +339,14 @@
             arrival(name, way, step).wait_recv()
             if step < 2:
                 send(name, way, step + 1)
-            elif name == LAST[way][-2]:
-                send(name, way, 3)
-                send(LAST[way][-1], way, 3)
-            elif name == LAST[way][0]:
-                send(name, way, 3)
+            elif (name, way) == ("q", 0):
+                send("q", 0, 3)
+                pl.when(chip != 7)(lambda: send("v", 0, 3))
+            elif (name, way) == ("m", 1):
+                send("m", 1, 3)
+                send("k", 1, 3)
+            elif (name, way) == ("v", 1):
+                pl.when(chip == 1)(lambda: send("v", 1, 3))
             give(name, way, step)
             if step == 0 and n in at_root:
                 pl.when(is_root)(at_root[n])
@@ -322,11 +370,23 @@
         norm_copy(twin).start()
         norm_copy(twin).wait_send()
 
-    for name, way in last[-2:]:
-        arrival(name, way, 3).wait_recv()
-        give(name, way, 3)
-    for way in (0, 1):
-        drain(send_sem.at[way], q_all.at[0:1792])
+    arrival("k", 1, 3).wait_recv()
+    give("k", 1, 3)
+
+    def end_up():
+        arrival("v", 0, 3).wait_recv()
+        give("v", 0, 3)
+
+    def end_down():
+        arrival("v", 1, 3).wait_recv()
+        give("v", 1, 3)
+
+    pl.when(jnp.logical_not(first))(end_up)
+    pl.when(first)(end_down)
+    pl.when(chip != 7)(lambda: drain(send_sem.at[0], q_all.at[0:1792]))
+    pl.when(chip == 7)(lambda: drain(send_sem.at[0], q_all.at[0:1728]))
+    pl.when(chip != 1)(lambda: drain(send_sem.at[1], q_all.at[0:1792]))
+    pl.when(chip == 1)(lambda: drain(send_sem.at[1], q_all.at[0:1856]))
     for kind in (0, 1):
         drain(hand_sem.at[kind], q_all.at[0:2048])
         drain(take_sem.at[kind], q_all.at[0:2048])
@@ -380,10 +440,11 @@
             pltpu.SemaphoreType.DMA((14,)),
             pltpu.SemaphoreType.DMA((2, 2)),
             pltpu.SemaphoreType.DMA((2,)),
-            pltpu.SemaphoreType.DMA((7 * len(PIECES),)),
+            pltpu.SemaphoreType.DMA((7 * len(PIECES) + 1,)),
             pltpu.SemaphoreType.DMA((2,)),
             pltpu.SemaphoreType.DMA((2,)),
             pltpu.SemaphoreType.DMA((6,)),
+            pltpu.SemaphoreType.REGULAR((2,)),
         ],
         compiler_params=pltpu.CompilerParams(
             collective_id=0, has_side_effects=True, vmem_limit_bytes=54400000

time: 75.3 us -> 74.3 us (0.987)
  Pallas kernels: 74.5 us -> 73.5 us
    pallas_call x1, Pallas kernels: 69.9 us -> 68.9 us  [on_device(): pl.pallas_call(gather_kernel, out_shape=(pltpu.VMEM((3072, 768), BF16), p...]
where the time goes in v4:
time: 74.3 us; the launch traced here: 74.1 us
  Pallas kernels  73.5 us (99%)
    pallas_call x1, Pallas kernels, on_device(): pl.pallas_call(gather_kernel, out_shape=(pltpu.VMEM((3072, 768), BF16), p...  68.9 us
    pallas_call x1, Pallas kernels, on_device(): pl.pallas_call(store_kernel, out_shape=(jax.ShapeDtypeStruct((3072, 768),...  4.64 us

profile of v4, /device:TPU:1, one launch (start us, length us, event | category | flops | bytes accessed | tf_op | source)
XLA Modules:
  0.0 74.1 jit_solution(12418835075037887112)
XLA Ops:
  0.6 68.9 %merge_and_gather.1 = (bf16[3072,768]{1,0:T(8,128)(2,1)S(1)}, bf16[3072,256]{1,0:T(8,128)(2,1)S(1)}, bf16[3072,256]{1,0:T(8,128)(2,1)S(1)}, bf16[8,768,384]{2,1,0:T(8,128)(2,1)S(1)}, bf16[24,128]{1,0:T(8,128)(2,1)S(1)}) custom-call(bf16[192,768]{1,0:T(8,128)(2,1)} %wq.1, bf16[32,192]{1,0:T(8,128)(2,1)} %bitcast.10, bf16[32,768]{1,0:T(8,128)(2,1)} %hq.1, ...), custom_call_target="tpu_custom_call" | custom-call | tf_op jit(solution)/shard_map/merge_and_gather/pallas_call | solution.py:412
  69.5 4.6 %store.1 = (bf16[3072,768]{1,0:T(8,128)(2,1)}, bf16[3072,256]{1,0:T(8,128)(2,1)}, bf16[3072,256]{1,0:T(8,128)(2,1)}, bf16[768,3072]{1,0:T(8,128)(2,1)}, bf16[24,128]{1,0:T(8,128)(2,1)}) custom-call(bf16[3072,768]{1,0:T(8,128)(2,1)S(1)} %get-tuple-element.15.q, bf16[3072,256]{1,0:T(8,128)(2,1)S(1)} %get-tuple-element.16.k, ...), custom_call_target="tpu_custom_call" | custom-call | tf_op jit(solution)/shard_map/store/pallas_call | solution.py:457

commit v5 on v4

v5 whole, which is shorter than its diff:
```python
import functools

import jax
import jax.numpy as jnp
from jax import lax
from jax.experimental import pallas as pl
from jax.experimental.pallas import tpu as pltpu
from jax.sharding import PartitionSpec as P

mix_rate = 2.0
MESH = pl.DeviceIdType.MESH
BF16 = jnp.bfloat16
F32 = jnp.float32

ROOT = 1
MIDDLE, MIDDLE_OF_4 = 192, 64


def merged(base, low_turned, high):
    delta = lax.dot_general(
        low_turned, high, (((0,), (0,)), ((), ())), preferred_element_type=F32
    )
    return (base.astype(F32) + mix_rate * delta).astype(BF16)


def gather_kernel(*refs):
    pl.run_scoped(
        functools.partial(gather, *refs),
        load_sem=pltpu.SemaphoreType.DMA((14,)),
        pair_sent=pltpu.SemaphoreType.DMA((2,)),
        send_sem=pltpu.SemaphoreType.DMA((2, 2)),
        hand_sem=pltpu.SemaphoreType.DMA((2,)),
        norm_sent=pltpu.SemaphoreType.DMA((3,)),
        pair_sem=pltpu.SemaphoreType.DMA((2,)),
        recv_sem=pltpu.SemaphoreType.DMA((2, 9)),
        take_sem=pltpu.SemaphoreType.DMA((2,)),
        norm_sem=pltpu.SemaphoreType.DMA((3,)),
        ready_sem=pltpu.SemaphoreType.REGULAR((2,)),
    )


def gather(
    wq, lq, hq, wk, lk, hk, wv, lv, hv, wm, lm, hm, nt, ns,
    w_all, m_all, n_out,
    wq_v, lq_v, hq_v, wk_v, lk_v, hk_v, wv_v, lv_v, hv_v, wm_v, lm_v, hm_v, nt_v, ns_v,
    n_all, n_wide,
    load_sem, pair_sent, send_sem, hand_sem, norm_sent,
    pair_sem, recv_sem, take_sem, norm_sem, ready_sem,
):
    zero = lax.axis_index("zero")
    col = lax.axis_index("cols")
    core = lax.rem(zero, 2)
    chip = lax.div(zero, 2)
    above = lax.rem(zero + 2, 16)
    below = lax.rem(zero + 14, 16)
    twin = zero + 1 - 2 * core

    half = pl.ds(pl.multiple_of(384 * core, 128), 384)
    other_half = pl.ds(pl.multiple_of(384 * (1 - core), 128), 384)
    my_rows = pl.ds(pl.multiple_of(192 * core, 64), 192)
    loads = [
        pltpu.make_async_copy(src, dst, load_sem.at[i])
        for i, (src, dst) in enumerate(
            (
                (lk, lk_v),
                (hk, hk_v),
                (wk, wk_v),
                (nt, nt_v),
                (ns, ns_v),
                (lv, lv_v),
                (hv, hv_v),
                (wv, wv_v),
                (lq, lq_v),
                (hq, hq_v),
                (wq, wq_v),
                (hm, hm_v.at[core]),
                (wm.at[:, half], wm_v.at[my_rows]),
                (lm.at[:, half], lm_v),
            )
        )
    ]
    for load in loads[:3]:
        load.start()

    barrier = pltpu.get_barrier_semaphore()

    def greet(peer):
        pl.semaphore_signal(
            barrier, inc=1, device_id={"zero": peer}, device_id_type=MESH
        )

    greet(twin)
    pl.when(chip != 7)(lambda: greet(above))
    pl.when(jnp.logical_or(chip == 0, chip >= 5))(lambda: greet(below))

    is_root = zero == ROOT

    @pl.when(is_root)
    def _():
        for other in range(16):
            if other != ROOT:
                greet(other)
        for far in (1, 2, 3):
            pl.semaphore_signal(
                barrier,
                inc=1,
                device_id={"cols": lax.rem(col + far, 4)},
                device_id_type=MESH,
            )

    for load in loads[3:]:
        load.start()

    def rows_of(origin, of, start=0, size=192):
        return pl.ds(pl.multiple_of(192 * (2 * origin + of) + start, 32), size)

    def slab(origin, of, start=0, size=384):
        return m_all.at[
            origin, pl.ds(pl.multiple_of(384 * of + start, 64), size)
        ]

    def piece(name, origin, way=0):
        if name == "k":
            return w_all.at[rows_of(origin, core), pl.ds(0, 256)]
        if name == "vq":
            return w_all.at[rows_of(origin, core), pl.ds(256, 1024)]
        if name == "w":
            return w_all.at[rows_of(origin, core)]
        if name == "m":
            return slab(origin, core)
        if name == "w half":
            return w_all.at[rows_of(origin, core, 96 * way, 96)]
        middle = MIDDLE_OF_4 if name == "m part of 4" else MIDDLE
        return slab(
            origin, core, middle * way, 384 - middle if way else middle
        )

    slots = {
        0: {"k": 0, "vq": 1, "m": 2},
        1: {"w": 3, "m": 4},
        2: {"w": 5, "m": 6},
        3: {"w half": 7, "m half": 8, "m part of 4": 8},
    }

    def arrived_from(way, step):
        return lax.rem(chip + (7 - step if way == 0 else step + 1), 8)

    def copy_of(name, way, step, origin, to):
        ref = piece(name, origin, way)
        return pltpu.make_async_remote_copy(
            src_ref=ref,
            dst_ref=ref,
            send_sem=send_sem.at[way, 1 if name[0] == "m" else 0],
            recv_sem=recv_sem.at[way, slots[step][name]],
            device_id={"zero": to},
            device_id_type=MESH,
        )

    def send(name, way, step):
        origin = chip if step == 0 else arrived_from(way, step - 1)
        copy_of(name, way, step, origin, above if way == 0 else below).start()

    def arrive(name, way, step):
        origin = arrived_from(way, step)
        copy_of(name, way, step, origin, twin).wait_recv()
        hand(name, origin, way)

    def hand(name, origin, way=0):
        ref = piece(name, origin, way)
        kind = 1 if name[0] == "m" else 0
        pltpu.make_async_remote_copy(
            src_ref=ref,
            dst_ref=ref,
            send_sem=hand_sem.at[kind],
            recv_sem=take_sem.at[kind],
            device_id={"zero": twin},
            device_id_type=MESH,
        ).start()

    def drain(sem, *refs):
        for ref in refs:
            pltpu.make_async_copy(ref, ref, sem).wait()

    own = rows_of(chip, core)
    for i in (0, 1, 2):
        loads[i].wait()
    w_all[own, 0:256] = merged(wk_v[...], lk_v[...], hk_v[...])
    loads[3].wait()
    loads[4].wait()
    n_all[col, zero] = jnp.zeros((1, 128), F32)
    n_all[col, zero, :, 0:48] = nt_v[...] + ns_v[...]
    row_copy = pltpu.make_async_remote_copy(
        src_ref=n_all.at[col, zero],
        dst_ref=n_all.at[col, zero],
        send_sem=norm_sent.at[0],
        recv_sem=norm_sem.at[0],
        device_id={"zero": ROOT},
        device_id_type=MESH,
    )
    pair = [
        pltpu.make_async_remote_copy(
            src_ref=src,
            dst_ref=dst,
            send_sem=pair_sent.at[i],
            recv_sem=pair_sem.at[i],
            device_id={"zero": twin},
            device_id_type=MESH,
        )
        for i, (src, dst) in enumerate(
            ((wm.at[:, other_half], wm_v.at[my_rows]), (hm, hm_v.at[core]))
        )
    ]
    pl.semaphore_wait(
        barrier,
        1
        + jnp.where(chip == 0, 0, 1)
        + jnp.where(chip >= 4, 1, 0)
        + jnp.where(is_root, 3, 1),
    )

    def ready(peer, i):
        pl.semaphore_signal(
            ready_sem.at[i], inc=1, device_id={"zero": peer}, device_id_type=MESH
        )

    pl.when(jnp.logical_and(chip >= 1, chip <= 4))(lambda: ready(below, 0))
    pl.when(chip == 7)(lambda: ready(above, 1))
    first = chip == 0
    early = jnp.logical_and(chip >= 1, chip <= 3)
    late = chip >= 4

    @pl.when(first)
    def _():
        pl.semaphore_wait(ready_sem.at[0], 1)
        send("k", 0, 0)

    @pl.when(jnp.logical_not(first))
    def _():
        send("k", 1, 0)

    pl.when(late)(lambda: send("k", 0, 0))
    for copy in pair:
        copy.start()
    for i in (5, 6, 7):
        loads[i].wait()
    w_all[own, 256:512] = merged(wv_v[...], lv_v[...], hv_v[...])
    for i in (8, 9, 10):
        loads[i].wait()
    w_all[own, 512:1280] = merged(wq_v[...], lq_v[...], hq_v[...])

    @pl.when(jnp.logical_not(first))
    def _():
        send("vq", 1, 0)

    @pl.when(early)
    def _():
        pl.semaphore_wait(ready_sem.at[0], 1)
        send("k", 0, 0)

    send("vq", 0, 0)

    @pl.when(first)
    def _():
        pl.semaphore_wait(ready_sem.at[1], 1)
        send("k", 1, 0)
        send("vq", 1, 0)

    @pl.when(jnp.logical_not(is_root))
    def _():
        row_copy.start()

    hand("w", chip)

    for i in (11, 12, 13):
        loads[i].wait()
    twin_rows = pl.ds(pl.multiple_of(192 * (1 - core), 64), 192)
    for i, dst in enumerate((wm_v.at[twin_rows], hm_v.at[1 - core])):
        pltpu.make_async_remote_copy(
            src_ref=dst,
            dst_ref=dst,
            send_sem=pair_sent.at[i],
            recv_sem=pair_sem.at[i],
            device_id={"zero": twin},
            device_id_type=MESH,
        ).wait_recv()
    row = lax.broadcasted_iota(jnp.int32, (192, 384), 0)
    lane = lax.broadcasted_iota(jnp.int32, (192, 384), 1)
    high = sum(
        jnp.dot(
            hm_v[c], (lane == row + 192 * c).astype(BF16), preferred_element_type=F32
        )
        for c in (0, 1)
    ).astype(BF16)
    for i in (0, 1, 2):
        lanes = slice(128 * i, 128 * i + 128)
        base = wm_v[:, lanes].astype(F32).T
        m_all[chip, pl.ds(pl.multiple_of(384 * core + 128 * i, 128), 128)] = merged(
            base, lm_v[:, lanes], high
        )
    send("m", 0, 0)
    send("m", 1, 0)
    hand("m", chip)
    for copy in pair:
        copy.wait_send()

    def meet_columns():
        drain(norm_sem.at[0], n_all.at[0, 0:15])
        for far in (1, 2, 3):
            pltpu.make_async_remote_copy(
                src_ref=n_all.at[col],
                dst_ref=n_all.at[col],
                send_sem=norm_sent.at[1],
                recv_sem=norm_sem.at[1],
                device_id={"cols": lax.rem(col + far, 4)},
                device_id_type=MESH,
            ).start()

    def assemble():
        drain(norm_sem.at[1], n_all.at[0:3])
        at = lax.broadcasted_iota(jnp.int32, (1, 128), 1)
        for g in range(8):
            e = [n_all[i % 4, 2 * g + i // 4] for i in range(8)]
            r = [pltpu.roll(e[i], (48 * i) % 128, 1) for i in range(8)]
            n_wide[3 * g : 3 * g + 1, :] = jnp.where(
                at < 48, r[0], jnp.where(at < 96, r[1], r[2])
            )
            n_wide[3 * g + 1 : 3 * g + 2, :] = jnp.where(
                at < 16,
                r[2],
                jnp.where(at < 64, r[3], jnp.where(at < 112, r[4], r[5])),
            )
            n_wide[3 * g + 2 : 3 * g + 3, :] = jnp.where(
                at < 32, r[5], jnp.where(at < 80, r[6], r[7])
            )
        n_out[...] = n_wide[...].astype(BF16)

    def norm_copy(to):
        return pltpu.make_async_remote_copy(
            src_ref=n_out,
            dst_ref=n_out,
            send_sem=norm_sent.at[2],
            recv_sem=norm_sem.at[2],
            device_id={"zero": to},
            device_id_type=MESH,
        )

    def spread():
        for to in (0, 2, 14, 4, 12, 6, 10, 8):
            norm_copy(to).start()

    ways = (0, 1)
    for way in ways:
        arrive("k", way, 0)
    pl.when(is_root)(meet_columns)
    for way in ways:
        arrive("vq", way, 0)
        send("w", way, 1)
    pl.when(is_root)(assemble)
    for way in ways:
        arrive("m", way, 0)
        send("m", way, 1)
    pl.when(is_root)(spread)
    for way in ways:
        arrive("w", way, 1)
        send("w", way, 2)
    for way in ways:
        arrive("m", way, 1)
        send("m", way, 2)
    for way in ways:
        arrive("w", way, 2)
        send("w half", way, 3)
    for way, odd_one in zip(ways, (7, 1)):
        arrive("m", way, 2)
        pl.when(chip != odd_one)(lambda: send("m half", way, 3))
        pl.when(chip == odd_one)(lambda: send("m part of 4", way, 3))
    for way in ways:
        arrive("w half", way, 3)

    @pl.when(is_root)
    def _():
        drain(norm_sent.at[1], n_all.at[0:3])
        drain(norm_sent.at[2], m_all.at[0, 0:64])

    @pl.when(jnp.logical_not(is_root))
    def _():
        row_copy.wait_send()
        norm_copy(twin).wait_recv()

    @pl.when(jnp.logical_and(core == 0, jnp.logical_not(first)))
    def _():
        norm_copy(twin).start()
        norm_copy(twin).wait_send()

    def finish(name):
        for way in ways:
            arrive(name, way, 3)

    pl.when(jnp.logical_not(first))(lambda: finish("m half"))
    pl.when(first)(lambda: finish("m part of 4"))
    for way, odd_one, rows in ((0, 7, 152), (1, 1, 184)):
        drain(send_sem.at[way, 0], w_all.at[0:672])
        pl.when(chip != odd_one)(
            lambda: drain(send_sem.at[way, 1], m_all.at[0:7, 0:192])
        )
        pl.when(chip == odd_one)(
            lambda: drain(send_sem.at[way, 1], m_all.at[:, 0:rows])
        )
    for sem in (hand_sem, take_sem):
        drain(sem.at[0], w_all.at[0:1536])
        drain(sem.at[1], m_all.at[:, 0:384])


def store_kernel(w, m, n, q_out, k_out, v_out, m_out, n_out, sem):
    parts = [(m.at[i], m_out.at[:, pl.ds(384 * i, 384)], 1) for i in range(8)]
    for i in range(4):
        rows = pl.ds(768 * i, 768)
        parts += [
            (w.at[rows, pl.ds(512, 768)], q_out.at[rows], 0),
            (w.at[rows, pl.ds(0, 256)], k_out.at[rows], 2),
            (w.at[rows, pl.ds(256, 256)], v_out.at[rows], 3),
        ]
    parts += [(n, n_out, 4)]
    for src, dst, i in parts:
        pltpu.make_async_copy(src, dst, sem.at[i]).start()
    for i, dst in enumerate((q_out, m_out, k_out, v_out, n_out)):
        pltpu.make_async_copy(dst, dst, sem.at[i]).wait()


def on_device(wq, lq, hq, wk, lk, hk, wv, lv, hv, wm, lm, hm, nt, ns):
    anywhere = pl.BlockSpec(memory_space=pltpu.HBM)
    onchip = pl.BlockSpec(memory_space=pltpu.VMEM)
    held = pl.pallas_call(
        gather_kernel,
        out_shape=(
            pltpu.VMEM((3072, 1280), BF16),
            pltpu.VMEM((8, 768, 384), BF16),
            pltpu.VMEM((24, 128), BF16),
        ),
        in_specs=[anywhere] * 14,
        out_specs=(onchip,) * 3,
        scratch_shapes=[
            pltpu.VMEM((192, 768), BF16),
            pltpu.VMEM((32, 192), BF16),
            pltpu.VMEM((32, 768), BF16),
            pltpu.VMEM((192, 256), BF16),
            pltpu.VMEM((32, 192), BF16),
            pltpu.VMEM((32, 256), BF16),
            pltpu.VMEM((192, 256), BF16),
            pltpu.VMEM((32, 192), BF16),
            pltpu.VMEM((32, 256), BF16),
            pltpu.VMEM((384, 384), BF16),
            pltpu.VMEM((32, 384), BF16),
            pltpu.VMEM((2, 32, 192), BF16),
            pltpu.VMEM((1, 48), F32),
            pltpu.VMEM((1, 48), F32),
            pltpu.VMEM((4, 16, 1, 128), F32),
            pltpu.VMEM((24, 128), F32),
        ],
        compiler_params=pltpu.CompilerParams(
            collective_id=0, has_side_effects=True, vmem_limit_bytes=54400000
        ),
        name="merge_and_gather",
    )(
        wq, lq.T, hq, wk, lk.T, hk, wv, lv.T, hv, wm.T, lm.T, hm,
        nt.reshape(1, 48), ns.reshape(1, 48),
    )
    q, k, v, m, norm = pl.pallas_call(
        store_kernel,
        out_shape=(
            jax.ShapeDtypeStruct((3072, 768), BF16),
            jax.ShapeDtypeStruct((3072, 256), BF16),
            jax.ShapeDtypeStruct((3072, 256), BF16),
            jax.ShapeDtypeStruct((768, 3072), BF16),
            jax.ShapeDtypeStruct((24, 128), BF16),
        ),
        in_specs=[onchip] * 3,
        out_specs=(anywhere,) * 5,
        scratch_shapes=[pltpu.SemaphoreType.DMA((5,))],
        compiler_params=pltpu.CompilerParams(vmem_limit_bytes=24 * 2**20),
        name="store",
    )(*held)
    return q, k, v, m, norm.reshape(3072)


def solution(mesh):
    placed = (
        P(("job", "zero"), "cols"),
        P(("job", "zero"), None),
        P("job", "cols"),
        P(("job", "zero"), "cols"),
        P(("job", "zero"), None),
        P("job", "cols"),
        P(("job", "zero"), "cols"),
        P(("job", "zero"), None),
        P("job", "cols"),
        P(("job", "cols"), "zero"),
        P(("job", "cols"), None),
        P("job", "zero"),
        P(("job", "zero", "cols")),
        P(("job", "zero", "cols")),
    )
    return jax.shard_map(
        on_device,
        mesh=mesh,
        in_specs=placed,
        out_specs=(
            P("job", "cols"),
            P("job", "cols"),
            P("job", "cols"),
            P(("job", "cols"), None),
            P("job"),
        ),
        check_vma=False,
    )
```

time: 74.3 us -> 72.9 us (0.981)
  Pallas kernels: 73.5 us -> 72.1 us
    pallas_call x1, Pallas kernels: 68.9 us -> 67.5 us  [on_device(): pl.pallas_call(gather_kernel, out_shape=(pltpu.VMEM((3072, 1280), BF16),...]
where the time goes in v5:
time: 72.9 us; the launch traced here: 72.8 us
  Pallas kernels  72.1 us (99%)
    pallas_call x1, Pallas kernels, on_device(): pl.pallas_call(gather_kernel, out_shape=(pltpu.VMEM((3072, 1280), BF16),...  67.5 us
    pallas_call x1, Pallas kernels, on_device(): pl.pallas_call(store_kernel, out_shape=(jax.ShapeDtypeStruct((3072, 768),...  4.58 us

profile of v5, /device:TPU:1, one launch (start us, length us, event | category | flops | bytes accessed | tf_op | source)
XLA Modules:
  0.0 72.8 jit_solution(4524556026064751732)
XLA Ops:
  0.6 67.5 %merge_and_gather.1 = (bf16[3072,1280]{1,0:T(8,128)(2,1)S(1)}, bf16[8,768,384]{2,1,0:T(8,128)(2,1)S(1)}, bf16[24,128]{1,0:T(8,128)(2,1)S(1)}) custom-call(bf16[192,768]{1,0:T(8,128)(2,1)} %refs_0_.1, bf16[32,192]{1,0:T(8,128)(2,1)} %bitcast.10, bf16[32,768]{1,0:T(8,128)(2,1)} %refs_2_.1, bf16[192,256]{1,0:T(8,128)(2,1)} %refs_3_.1, ...), custom_call_target="tpu_custom_call" | custom-call | tf_op jit(solution)/shard_map/merge_and_gather/pallas_call | solution.py:432
  68.2 4.6 %store.1 = (bf16[3072,768]{1,0:T(8,128)(2,1)}, bf16[3072,256]{1,0:T(8,128)(2,1)}, bf16[3072,256]{1,0:T(8,128)(2,1)}, bf16[768,3072]{1,0:T(8,128)(2,1)}, bf16[24,128]{1,0:T(8,128)(2,1)}) custom-call(bf16[3072,1280]{1,0:T(8,128)(2,1)S(1)} %get-tuple-element.13.w, bf16[8,768,384]{2,1,0:T(8,128)(2,1)S(1)} %get-tuple-element.14.m, ...), custom_call_target="tpu_custom_call" | custom-call | tf_op jit(solution)/shard_map/store/pallas_call | solution.py:467

commit v6 on v5

--- a/solution.py
+++ b/solution.py
@@ -185,6 +185,50 @@
     for i in (0, 1, 2):
         loads[i].wait()
     w_all[own, 0:256] = merged(wk_v[...], lk_v[...], hk_v[...])
+    pair = [
+        pltpu.make_async_remote_copy(
+            src_ref=src,
+            dst_ref=dst,
+            send_sem=pair_sent.at[i],
+            recv_sem=pair_sem.at[i],
+            device_id={"zero": twin},
+            device_id_type=MESH,
+        )
+        for i, (src, dst) in enumerate(
+            ((wm.at[:, other_half], wm_v.at[my_rows]), (hm, hm_v.at[core]))
+        )
+    ]
+    pl.semaphore_wait(
+        barrier,
+        1
+        + jnp.where(chip == 0, 0, 1)
+        + jnp.where(chip >= 4, 1, 0)
+        + jnp.where(is_root, 3, 1),
+    )
+
+    def ready(peer, i):
+        pl.semaphore_signal(
+            ready_sem.at[i], inc=1, device_id={"zero": peer}, device_id_type=MESH
+        )
+
+    pl.when(jnp.logical_and(chip >= 1, chip <= 4))(lambda: ready(below, 0))
+    pl.when(chip == 7)(lambda: ready(above, 1))
+    first = chip == 0
+    early = jnp.logical_and(chip >= 1, chip <= 3)
+    late = chip >= 4
+
+    @pl.when(first)
+    def _():
+        pl.semaphore_wait(ready_sem.at[0], 1)
+        send("k", 0, 0)
+
+    @pl.when(jnp.logical_not(first))
+    def _():
+        send("k", 1, 0)
+
+    pl.when(late)(lambda: send("k", 0, 0))
+    for copy in pair:
+        copy.start()
     loads[3].wait()
     loads[4].wait()
     n_all[col, zero] = jnp.zeros((1, 128), F32)
@@ -197,50 +241,6 @@
         device_id={"zero": ROOT},
         device_id_type=MESH,
     )
-    pair = [
-        pltpu.make_async_remote_copy(
-            src_ref=src,
-            dst_ref=dst,
-            send_sem=pair_sent.at[i],
-            recv_sem=pair_sem.at[i],
-            device_id={"zero": twin},
-            device_id_type=MESH,
-        )
-        for i, (src, dst) in enumerate(
-            ((wm.at[:, other_half], wm_v.at[my_rows]), (hm, hm_v.at[core]))
-        )
-    ]
-    pl.semaphore_wait(
-        barrier,
-        1
-        + jnp.where(chip == 0, 0, 1)
-        + jnp.where(chip >= 4, 1, 0)
-        + jnp.where(is_root, 3, 1),
-    )
-
-    def ready(peer, i):
-        pl.semaphore_signal(
-            ready_sem.at[i], inc=1, device_id={"zero": peer}, device_id_type=MESH
-        )
-
-    pl.when(jnp.logical_and(chip >= 1, chip <= 4))(lambda: ready(below, 0))
-    pl.when(chip == 7)(lambda: ready(above, 1))
-    first = chip == 0
-    early = jnp.logical_and(chip >= 1, chip <= 3)
-    late = chip >= 4
-
-    @pl.when(first)
-    def _():
-        pl.semaphore_wait(ready_sem.at[0], 1)
-        send("k", 0, 0)
-
-    @pl.when(jnp.logical_not(first))
-    def _():
-        send("k", 1, 0)
-
-    pl.when(late)(lambda: send("k", 0, 0))
-    for copy in pair:
-        copy.start()
     for i in (5, 6, 7):
         loads[i].wait()
     w_all[own, 256:512] = merged(wv_v[...], lv_v[...], hv_v[...])
@@ -410,7 +410,13 @@
         drain(sem.at[1], m_all.at[:, 0:384])
 
 
-def store_kernel(w, m, n, q_out, k_out, v_out, m_out, n_out, sem):
+def store_kernel(*refs):
+    pl.run_scoped(
+        functools.partial(store, *refs), sem=pltpu.SemaphoreType.DMA((5,))
+    )
+
+
+def store(w, m, n, q_out, k_out, v_out, m_out, n_out, sem):
     parts = [(m.at[i], m_out.at[:, pl.ds(384 * i, 384)], 1) for i in range(8)]
     for i in range(4):
         rows = pl.ds(768 * i, 768)
@@ -475,7 +481,6 @@
         ),
         in_specs=[onchip] * 3,
         out_specs=(anywhere,) * 5,
-        scratch_shapes=[pltpu.SemaphoreType.DMA((5,))],
         compiler_params=pltpu.CompilerParams(vmem_limit_bytes=24 * 2**20),
         name="store",
     )(*held)

time: 72.9 us -> 72.9 us (level)
  no operation moved by 1% of the time
where the time goes in v6:
time: 72.9 us; the launch traced here: 72.7 us
  Pallas kernels  72.1 us (99%)
    pallas_call x1, Pallas kernels, on_device(): pl.pallas_call(gather_kernel, out_shape=(pltpu.VMEM((3072, 1280), BF16),...  67.5 us
    pallas_call x1, Pallas kernels, on_device(): pl.pallas_call(store_kernel, out_shape=(jax.ShapeDtypeStruct((3072, 768),...  4.54 us

profile of v6, /device:TPU:1, one launch (start us, length us, event | category | flops | bytes accessed | tf_op | source)
XLA Modules:
  0.0 72.7 jit_solution(4139284129294918506)
XLA Ops:
  0.6 67.5 %merge_and_gather.1 = (bf16[3072,1280]{1,0:T(8,128)(2,1)S(1)}, bf16[8,768,384]{2,1,0:T(8,128)(2,1)S(1)}, bf16[24,128]{1,0:T(8,128)(2,1)S(1)}) custom-call(bf16[192,768]{1,0:T(8,128)(2,1)} %refs_0_.1, bf16[32,192]{1,0:T(8,128)(2,1)} %bitcast.10, bf16[32,768]{1,0:T(8,128)(2,1)} %refs_2_.1, bf16[192,256]{1,0:T(8,128)(2,1)} %refs_3_.1, ...), custom_call_target="tpu_custom_call" | custom-call | tf_op jit(solution)/shard_map/merge_and_gather/pallas_call | solution.py:438
  68.2 4.5 %store.1 = (bf16[3072,768]{1,0:T(8,128)(2,1)}, bf16[3072,256]{1,0:T(8,128)(2,1)}, bf16[3072,256]{1,0:T(8,128)(2,1)}, bf16[768,3072]{1,0:T(8,128)(2,1)}, bf16[24,128]{1,0:T(8,128)(2,1)}) custom-call(bf16[3072,1280]{1,0:T(8,128)(2,1)S(1)} %get-tuple-element.13.refs_0_, bf16[8,768,384]{2,1,0:T(8,128)(2,1)S(1)} %get-tuple-element.14.refs_1_, ...), custom_call_target="tpu_custom_call" | custom-call | tf_op jit(solution)/shard_map/store/pallas_call | solution.py:473

commit v7 on v6

--- a/solution.py
+++ b/solution.py
@@ -13,7 +13,9 @@
 F32 = jnp.float32
 
 ROOT = 1
-MIDDLE, MIDDLE_OF_4 = 192, 64
+SPLIT = {4: 80, 3: 320}
+EVEN = 192
+END = 64
 
 
 def merged(base, low_turned, high):
@@ -32,7 +34,7 @@
         hand_sem=pltpu.SemaphoreType.DMA((2,)),
         norm_sent=pltpu.SemaphoreType.DMA((3,)),
         pair_sem=pltpu.SemaphoreType.DMA((2,)),
-        recv_sem=pltpu.SemaphoreType.DMA((2, 9)),
+        recv_sem=pltpu.SemaphoreType.DMA((2, 10)),
         take_sem=pltpu.SemaphoreType.DMA((2,)),
         norm_sem=pltpu.SemaphoreType.DMA((3,)),
         ready_sem=pltpu.SemaphoreType.REGULAR((2,)),
@@ -116,7 +118,7 @@
 
     def slab(origin, of, start=0, size=384):
         return m_all.at[
-            origin, pl.ds(pl.multiple_of(384 * of + start, 64), size)
+            origin, pl.ds(pl.multiple_of(384 * of + start, 16), size)
         ]
 
     def piece(name, origin, way=0):
@@ -130,16 +132,27 @@
             return slab(origin, core)
         if name == "w half":
             return w_all.at[rows_of(origin, core, 96 * way, 96)]
-        middle = MIDDLE_OF_4 if name == "m part of 4" else MIDDLE
-        return slab(
-            origin, core, middle * way, 384 - middle if way else middle
-        )
+        start, size = last_rows(name, way)
+        if name.endswith("end"):
+            return slab(origin, core, start + size - END, END)
+        return slab(origin, core, start, size - END)
+
+    def last_rows(name, way):
+        split = int(name.split()[1])
+        return (split, 384 - split) if way else (0, split)
+
+    def by_origin(origin, act):
+        odd = origin < 0
+        for o, split in SPLIT.items():
+            pl.when(origin == o)(functools.partial(act, split))
+            odd = jnp.logical_or(odd, origin == o)
+        pl.when(jnp.logical_not(odd))(functools.partial(act, EVEN))
 
     slots = {
         0: {"k": 0, "vq": 1, "m": 2},
         1: {"w": 3, "m": 4},
         2: {"w": 5, "m": 6},
-        3: {"w half": 7, "m half": 8, "m part of 4": 8},
+        3: {"w half": 7},
     }
 
     def arrived_from(way, step):
@@ -151,7 +164,7 @@
             src_ref=ref,
             dst_ref=ref,
             send_sem=send_sem.at[way, 1 if name[0] == "m" else 0],
-            recv_sem=recv_sem.at[way, slots[step][name]],
+            recv_sem=recv_sem.at[way, slots[step].get(name, 9 if "end" in name else 8)],
             device_id={"zero": to},
             device_id_type=MESH,
         )
@@ -348,6 +361,15 @@
         for to in (0, 2, 14, 4, 12, 6, 10, 8):
             norm_copy(to).start()
 
+    def send_last(way, split):
+        for end in ("", " end"):
+            if end or last_rows(f"m {split}", way)[1] > END:
+                send(f"m {split}{end}", way, 3)
+
+    def arrive_last(way, end, split):
+        if end or last_rows(f"m {split}", way)[1] > END:
+            arrive(f"m {split}{end}", way, 3)
+
     ways = (0, 1)
     for way in ways:
         arrive("k", way, 0)
@@ -369,10 +391,9 @@
     for way in ways:
         arrive("w", way, 2)
         send("w half", way, 3)
-    for way, odd_one in zip(ways, (7, 1)):
+    for way in ways:
         arrive("m", way, 2)
-        pl.when(chip != odd_one)(lambda: send("m half", way, 3))
-        pl.when(chip == odd_one)(lambda: send("m part of 4", way, 3))
+        by_origin(arrived_from(way, 2), functools.partial(send_last, way))
     for way in ways:
         arrive("w half", way, 3)
 
@@ -391,32 +412,26 @@
         norm_copy(twin).start()
         norm_copy(twin).wait_send()
 
-    def finish(name):
+    for end in ("", " end"):
         for way in ways:
-            arrive(name, way, 3)
-
-    pl.when(jnp.logical_not(first))(lambda: finish("m half"))
-    pl.when(first)(lambda: finish("m part of 4"))
-    for way, odd_one, rows in ((0, 7, 152), (1, 1, 184)):
+            by_origin(
+                arrived_from(way, 3), functools.partial(arrive_last, way, end)
+            )
+
+    def drain_slabs(way, split):
+        rows = 3 * 384 + last_rows(f"m {split}", way)[1]
+        parts = next(p for p in (8, 6, 4, 2) if rows % (8 * p) == 0)
+        drain(send_sem.at[way, 1], m_all.at[0:parts, 0 : rows // parts])
+
+    for way in ways:
         drain(send_sem.at[way, 0], w_all.at[0:672])
-        pl.when(chip != odd_one)(
-            lambda: drain(send_sem.at[way, 1], m_all.at[0:7, 0:192])
-        )
-        pl.when(chip == odd_one)(
-            lambda: drain(send_sem.at[way, 1], m_all.at[:, 0:rows])
-        )
+        by_origin(arrived_from(way, 2), functools.partial(drain_slabs, way))
     for sem in (hand_sem, take_sem):
         drain(sem.at[0], w_all.at[0:1536])
         drain(sem.at[1], m_all.at[:, 0:384])
 
 
-def store_kernel(*refs):
-    pl.run_scoped(
-        functools.partial(store, *refs), sem=pltpu.SemaphoreType.DMA((5,))
-    )
-
-
-def store(w, m, n, q_out, k_out, v_out, m_out, n_out, sem):
+def store_kernel(w, m, n, q_out, k_out, v_out, m_out, n_out, sem):
     parts = [(m.at[i], m_out.at[:, pl.ds(384 * i, 384)], 1) for i in range(8)]
     for i in range(4):
         rows = pl.ds(768 * i, 768)
@@ -481,6 +496,7 @@
         ),
         in_specs=[onchip] * 3,
         out_specs=(anywhere,) * 5,
+        scratch_shapes=[pltpu.SemaphoreType.DMA((5,))],
         compiler_params=pltpu.CompilerParams(vmem_limit_bytes=24 * 2**20),
         name="store",
     )(*held)

time: 72.9 us -> 73.1 us (level)
  no operation moved by 1% of the time
where the time goes in v7:
time: 73.1 us; the launch traced here: 72.9 us
  Pallas kernels  72.2 us (99%)
    pallas_call x1, Pallas kernels, on_device(): pl.pallas_call(gather_kernel, out_shape=(pltpu.VMEM((3072, 1280), BF16),...  67.7 us
    pallas_call x1, Pallas kernels, on_device(): pl.pallas_call(store_kernel, out_shape=(jax.ShapeDtypeStruct((3072, 768),...  4.58 us

profile of v7, /device:TPU:1, one launch (start us, length us, event | category | flops | bytes accessed | tf_op | source)
XLA Modules:
  0.0 72.9 jit_solution(3462947434734228270)
XLA Ops:
  0.6 67.7 %merge_and_gather.1 = (bf16[3072,1280]{1,0:T(8,128)(2,1)S(1)}, bf16[8,768,384]{2,1,0:T(8,128)(2,1)S(1)}, bf16[24,128]{1,0:T(8,128)(2,1)S(1)}) custom-call(bf16[192,768]{1,0:T(8,128)(2,1)} %refs_0_.1, bf16[32,192]{1,0:T(8,128)(2,1)} %bitcast.10, bf16[32,768]{1,0:T(8,128)(2,1)} %refs_2_.1, bf16[192,256]{1,0:T(8,128)(2,1)} %refs_3_.1, ...), custom_call_target="tpu_custom_call" | custom-call | tf_op jit(solution)/shard_map/merge_and_gather/pallas_call | solution.py:453
  68.3 4.6 %store.1 = (bf16[3072,768]{1,0:T(8,128)(2,1)}, bf16[3072,256]{1,0:T(8,128)(2,1)}, bf16[3072,256]{1,0:T(8,128)(2,1)}, bf16[768,3072]{1,0:T(8,128)(2,1)}, bf16[24,128]{1,0:T(8,128)(2,1)}) custom-call(bf16[3072,1280]{1,0:T(8,128)(2,1)S(1)} %get-tuple-element.13.w, bf16[8,768,384]{2,1,0:T(8,128)(2,1)S(1)} %get-tuple-element.14.m, ...), custom_call_target="tpu_custom_call" | custom-call | tf_op jit(solution)/shard_map/store/pallas_call | solution.py:488

commit v8 on v5

--- a/solution.py
+++ b/solution.py
@@ -411,15 +411,19 @@
 
 
 def store_kernel(w, m, n, q_out, k_out, v_out, m_out, n_out, sem):
-    parts = [(m.at[i], m_out.at[:, pl.ds(384 * i, 384)], 1) for i in range(8)]
-    for i in range(4):
-        rows = pl.ds(768 * i, 768)
+    parts = [(n, n_out, 4)]
+    for i in range(16):
+        rows, slab_rows = pl.ds(192 * i, 192), pl.ds(384 * (i % 2), 384)
         parts += [
             (w.at[rows, pl.ds(512, 768)], q_out.at[rows], 0),
+            (
+                m.at[i // 2, slab_rows],
+                m_out.at[slab_rows, pl.ds(384 * (i // 2), 384)],
+                1,
+            ),
             (w.at[rows, pl.ds(0, 256)], k_out.at[rows], 2),
             (w.at[rows, pl.ds(256, 256)], v_out.at[rows], 3),
         ]
-    parts += [(n, n_out, 4)]
     for src, dst, i in parts:
         pltpu.make_async_copy(src, dst, sem.at[i]).start()
     for i, dst in enumerate((q_out, m_out, k_out, v_out, n_out)):

time: 72.9 us -> 72.9 us (level)
  no operation moved by 1% of the time
where the time goes in v8:
time: 72.9 us; the launch traced here: 72.7 us
  Pallas kernels  72.1 us (99%)
    pallas_call x1, Pallas kernels, on_device(): pl.pallas_call(gather_kernel, out_shape=(pltpu.VMEM((3072, 1280), BF16),...  67.5 us
    pallas_call x1, Pallas kernels, on_device(): pl.pallas_call(store_kernel, out_shape=(jax.ShapeDtypeStruct((3072, 768),...  4.55 us

profile of v8, /device:TPU:1, one launch (start us, length us, event | category | flops | bytes accessed | tf_op | source)
XLA Modules:
  0.0 72.7 jit_solution(11237518904764613689)
XLA Ops:
  0.6 67.5 %merge_and_gather.1 = (bf16[3072,1280]{1,0:T(8,128)(2,1)S(1)}, bf16[8,768,384]{2,1,0:T(8,128)(2,1)S(1)}, bf16[24,128]{1,0:T(8,128)(2,1)S(1)}) custom-call(bf16[192,768]{1,0:T(8,128)(2,1)} %refs_0_.1, bf16[32,192]{1,0:T(8,128)(2,1)} %bitcast.10, bf16[32,768]{1,0:T(8,128)(2,1)} %refs_2_.1, bf16[192,256]{1,0:T(8,128)(2,1)} %refs_3_.1, ...), custom_call_target="tpu_custom_call" | custom-call | tf_op jit(solution)/shard_map/merge_and_gather/pallas_call | solution.py:436
  68.2 4.6 %store.1 = (bf16[3072,768]{1,0:T(8,128)(2,1)}, bf16[3072,256]{1,0:T(8,128)(2,1)}, bf16[3072,256]{1,0:T(8,128)(2,1)}, bf16[768,3072]{1,0:T(8,128)(2,1)}, bf16[24,128]{1,0:T(8,128)(2,1)}) custom-call(bf16[3072,1280]{1,0:T(8,128)(2,1)S(1)} %get-tuple-element.13.w, bf16[8,768,384]{2,1,0:T(8,128)(2,1)S(1)} %get-tuple-element.14.m, ...), custom_call_target="tpu_custom_call" | custom-call | tf_op jit(solution)/shard_map/store/pallas_call | solution.py:471
